TPU v7x, 512 devices: a whole 4x8x8 slice. The times are simulated.
512 devices in a mesh: row: 32 (over z, x), col: 16 (over y, core).
Axes of the slice: x: 4, y: 8, z: 8, core: 2. Of those that a mesh axis runs over, the one named last changes fastest.
Arguments:
- dense_a: bfloat16 [1024, 512, 512], P(('row', 'col')), may hold values from -6 to 6
- dense_b: bfloat16 [1024, 512, 512], P(('row', 'col')), may hold values from -0.25 to 0.25
- inner_basis_stack: bfloat16 [1024, 2, 512, 128], P(('row', 'col')), may hold values from -0.25 to 0.25
- outer_basis_stack: bfloat16 [1024, 2, 512, 128], P(('row', 'col')), may hold values from -1 to 1
- ascent: bfloat16 [512, 4, 2, 128, 128], P(('row', 'col')), may hold values from -0.4375 to 0.4375
- descent: bfloat16 [512, 4, 2, 128, 128], P(('row', 'col')), may hold values from -0.5 to 0.5
- couplings: bfloat16 [512, 2, 4, 128, 128], P(('row', 'col')), may hold values from -0.5 to 0.5
Outputs:
- product_diag: bfloat16 [1024, 512, 512], P(('row', 'col'))
All inputs are finite; a program needn't handle non-finite values.
Results may differ from a plain program's by a relative error of at most 0.015.
Values may be sent and summed in bfloat16 or wider, within the bound.
A program may use at most 64 MiB of HBM per device.

v0:
```python
import jax
import jax.numpy as jnp
from jax import lax
from jax.sharding import PartitionSpec as P

HIGHEST_PRECISION = lax.Precision.HIGHEST


def laid_out(blocks, dim):
    blocks = jnp.moveaxis(blocks, 0, dim)
    dims = blocks.shape
    return blocks.reshape(*dims[:dim], dims[dim] * dims[dim + 1], *dims[dim + 2 :])


def from_everyone(array, axis):
    copies = jnp.broadcast_to(array, (lax.axis_size(axis), *array.shape))
    return lax.all_to_all(copies, axis, split_axis=0, concat_axis=0, tiled=True)


def gather_directly(array, axis, dim):
    return laid_out(from_everyone(array, axis), dim)


def sent_together(arrays, axis, dim, along):
    both = jnp.concatenate(arrays, axis=along)
    filled, at, finished = (gather_directly(both, axis, dim), 0, [])
    for a in arrays:
        finished.append(lax.slice_in_dim(filled, at, at + a.shape[along], axis=along))
        at += a.shape[along]
    return tuple(finished)


def from_partner(block, axis, distance):
    count = lax.axis_size(axis)
    route = []
    for low in range(count):
        high = low | 1 << distance
        if high != low and high < count:
            route += [(low, high), (high, low)]
    return lax.ppermute(block, axis, route)


def multiply(first_arg, second_arg):
    return jnp.matmul(
        first_arg.astype(jnp.float32), second_arg.astype(jnp.float32), precision=HIGHEST_PRECISION
    )


def lifted(pair_stack, inner_value):
    return multiply(multiply(jnp.swapaxes(pair_stack[:, 0], 1, 2), inner_value), pair_stack[:, 1])


def lowered(pair_stack, parent):
    return multiply(multiply(pair_stack[:, 0], parent), jnp.swapaxes(pair_stack[:, 1], 1, 2))


def lift_single(up_pair, inner_value):
    return multiply(multiply(up_pair[0].T, inner_value), up_pair[1])


def lower_single(down_pair, parent):
    return multiply(multiply(down_pair[0], parent), down_pair[1].T)


def sibling_terms(blocks, inner_value):
    left_terms = multiply(multiply(blocks[:, 0], inner_value[1::2]), blocks[:, 3])
    right_terms = multiply(multiply(blocks[:, 1], inner_value[0::2]), blocks[:, 2])
    return jnp.stack([left_terms, right_terms], 1).reshape(inner_value.shape)


def owners(stacked, height):
    return stacked[2 ** (height - 1) - 1 :: 2**height]


def ancestor_owners(position, levels):
    powers = 2 ** jnp.arange(levels, dtype=jnp.int32)
    return position // (2 * powers) * (2 * powers) + powers - 1


def shards(dense_a, dense_b, inner_basis_stack, outer_basis_stack, ascent, descent, couplings):
    rank_size = ascent.shape[-1]
    up_pairs = ascent[0]
    down_pairs = descent[0]
    blocks = couplings[0]
    leaf_inner_product = jnp.einsum(
        "ufw,ufa->uwa",
        inner_basis_stack[:, 0],
        inner_basis_stack[:, 1],
        preferred_element_type=jnp.float32,
    )
    leaf_terms = lifted(up_pairs[0:2], leaf_inner_product)
    node_inner = leaf_terms[0] + leaf_terms[1]
    node_term = lift_single(up_pairs[2], node_inner)
    levels = (lax.axis_size("row") * lax.axis_size("col")).bit_length() - 1
    group_height = lax.axis_size("col").bit_length() - 1
    position = lax.axis_index(("row", "col"))
    own_gens = jnp.concatenate([up_pairs[3], down_pairs[3], blocks[1]], 0)
    owner_list = ancestor_owners(position, levels)
    sibling_inner = []
    first_height = 1
    group_inner, group_term = tuple(
        (
            part.astype(jnp.float32)
            for part in sent_together(
                (node_inner[None].astype(jnp.bfloat16), node_term[None].astype(jnp.bfloat16)),
                "col",
                0,
                1,
            )
        )
    )
    group_gens = lax.all_gather(own_gens[None], "col", axis=0, tiled=True)
    column = lax.axis_index("col")
    group_count = group_gens.shape[0]
    members = position - column + jnp.arange(group_count, dtype=jnp.int32)
    pick = (owner_list[:, None] == members[None, :]).astype(jnp.bfloat16)
    table = jnp.einsum(
        "lc,cgij->lgij", pick, group_gens, preferred_element_type=jnp.float32
    ).astype(jnp.bfloat16)
    current_inner = group_inner
    current_term = group_term
    for height in range(1, group_height + 1):
        own_index = column // 2 ** (height - 1)
        other_index = own_index + 1 - 2 * (own_index % 2)
        sibling_inner.append(lax.dynamic_index_in_dim(current_inner, other_index, 0, False))
        current_inner = current_term[0::2] + current_term[1::2]
        current_term = lifted(owners(group_gens[:, 0:2], height), current_inner)
    node_inner = current_inner[0]
    node_term = current_term[0]
    first_height = group_height + 1
    for height in range(first_height, levels + 1):
        upper_part = table[height - 1 :]
        outgoing = jnp.stack([node_inner, node_term])
        received = from_partner(
            outgoing.astype(jnp.bfloat16), "row", height - 1 - group_height
        ).astype(outgoing.dtype)
        got_gens = from_partner(upper_part, "row", height - 1 - group_height)
        table = jnp.concatenate([table[: height - 1], upper_part + got_gens], 0)
        sibling_inner.append(received[0])
        node_inner = node_term + received[1]
        if height < levels:
            node_term = lift_single(table[height - 1, 0:2], node_inner)
    own_coupling = jnp.zeros((rank_size, rank_size), jnp.float32)
    for height in range(levels, 0, -1):
        blocks_here = table[height - 1, 4:8]
        on_left = position // 2 ** (height - 1) % 2 == 0
        first_block = jnp.where(on_left, blocks_here[0], blocks_here[1])
        second_block = jnp.where(on_left, blocks_here[3], blocks_here[2])
        near_value = multiply(multiply(first_block, sibling_inner[height - 1]), second_block)
        if height >= 2:
            down_here = table[height - 2, 2:4]
        else:
            down_here = down_pairs[2]
        own_coupling = near_value + lower_single(down_here, own_coupling)
    near_leaves = sibling_terms(blocks[0][None], leaf_inner_product)
    spread_leaves = jnp.broadcast_to(own_coupling, (2, rank_size, rank_size))
    leaf_coupling = near_leaves + lowered(down_pairs[0:2], spread_leaves)
    rounded_count = leaf_coupling.astype(jnp.bfloat16)
    spread_rows = jnp.einsum(
        "ywv,yvu->ywu", outer_basis_stack[:, 0], rounded_count, preferred_element_type=jnp.float32
    ).astype(jnp.bfloat16)
    result_block = jnp.einsum("lij,ljk->lik", dense_a, dense_b, preferred_element_type=jnp.float32)
    result_block = result_block + jnp.einsum(
        "lms,lns->lmn", spread_rows, outer_basis_stack[:, 1], preferred_element_type=jnp.float32
    )
    return result_block.astype(jnp.bfloat16)


def solution(mesh):
    placed = (
        P(("row", "col"), None, None),
        P(("row", "col"), None, None),
        P(("row", "col"), None, None, None),
        P(("row", "col"), None, None, None),
        P(("row", "col"), None, None, None, None),
        P(("row", "col"), None, None, None, None),
        P(("row", "col"), None, None, None, None),
    )
    return jax.shard_map(
        shards, mesh=mesh, in_specs=placed, out_specs=P(("row", "col"), None, None), check_vma=False
    )
```

profile of v0, /device:TPU:1, one launch (start us, length us, event | category | flops | bytes accessed | tf_op | source)
XLA Modules:
  0.0 263.0 jit_solution(3073001828344682090)
XLA Ops:
  11.0 1.3 fusion.11
  16.0 10.3 %all-to-all-start = ((bf16[16,1,256,128]{3,2,1,0:T(8,128)(2,1)}), bf16[16,1,256,128]{3,2,1,0:T(8,128)(2,1)S(1)}, u32[]{:S(2)}, u32[]{:S(2)}) async-start(bf16[16,1,256,128]{3,2,1,0:T(8,128)(2,1)} %broadcast_in_dim.25), calls=%async_computation | async-start | bytes 2097152 | tf_op jit(solution)/shard_map/all_to_all | solution.py:17
  27.5 36.0 %all-to-all-done = bf16[16,1,256,128]{3,2,1,0:T(8,128)(2,1)S(1)} async-done(((bf16[16,1,256,128]{3,2,1,0:T(8,128)(2,1)}), bf16[16,1,256,128]{3,2,1,0:T(8,128)(2,1)S(1)}, u32[]{:S(2)}, u32[]{:S(2)}) %all-to-all-start) | async-done | bytes 1048608 | tf_op jit(solution)/shard_map/all_to_all | solution.py:17
  63.7 14.0 %all-gather.3.cloned.1.call-done = bf16[128,128,128]{2,1,0:T(8,128)(2,1)} async-done(((bf16[8,128,128]{2,1,0:T(8,128)(2,1)}), bf16[128,128,128]{2,1,0:T(8,128)(2,1)}) %all-gather.3.cloned.1.call-update) | async-done | bytes 4194320 | tf_op jit(solution)/shard_map/all_gather | solution.py:112
  77.7 1.3 slice.952
  81.7 1.9 collective-permute-start.1
  83.6 2.8 %fusion.2 = bf16[9,8,128,128]{3,0,2,1:T(8,128)(2,1)S(1)} fusion(bf16[16,8,128,128]{3,2,1,0:T(8,128)(2,1)S(1)} %bitcast.385, s32[16]{0:T(128)S(1)} %iota_add_fusion, s32[9]{0:T(128)S(1)} %add_add_fusion), kind=kOutput, calls=%fused_computation.2 | convolution fusion | flops 38928528 | bytes 6553700 | tf_op jit(solution)/shard_map/lc,cgij->lgij/dot_general | solution.py:117
  88.9 3.5 %collective-permute-start = (bf16[5,8,128,128]{3,2,1,0:T(8,128)(2,1)S(1)}, bf16[5,8,128,128]{3,2,1,0:T(8,128)(2,1)S(1)}, u32[]{:S(2)}, u32[]{:S(2)}) collective-permute-start(bf16[5,8,128,128]{3,2,1,0:T(8,128)(2,1)S(1)} %copy.51), channel_id=1, source_target_pairs={{0,16},{16,0},{32,48},{48,32},{64,80},{80,64},{96,112},{112,96},{1... | collective-permute-start | bytes 3932168 | tf_op jit(solution)/shard_map/ppermute | solution.py:40
  93.9 26.9 %collective-permute-done = bf16[5,8,128,128]{3,2,1,0:T(8,128)(2,1)S(1)} collective-permute-done((bf16[5,8,128,128]{3,2,1,0:T(8,128)(2,1)S(1)}, bf16[5,8,128,128]{3,2,1,0:T(8,128)(2,1)S(1)}, u32[]{:S(2)}, u32[]{:S(2)}) %collective-permute-start) | collective-permute-done | bytes 1310752 | tf_op jit(solution)/shard_map/ppermute | solution.py:40
  120.8 1.3 copy_add_fusion
  122.9 3.5 %collective-permute-start.2 = (bf16[4,8,128,128]{3,0,2,1:T(4,128)(2,1)S(1)}, bf16[4,8,128,128]{3,0,2,1:T(4,128)(2,1)S(1)}, u32[]{:S(2)}, u32[]{:S(2)}) collective-permute-start(bf16[4,8,128,128]{3,0,2,1:T(4,128)(2,1)S(1)} %slice.978), channel_id=1, source_target_pairs={{0,32},{32,0},{16,48},{48,16},{64,96},{96,64},{80,112},{112,80},{1... | collective-permute-start | bytes 3145736 | tf_op jit(solution)/shard_map/ppermute | solution.py:40
  126.9 3.3 %collective-permute-start.3 = (bf16[2,128,128]{2,1,0:T(8,128)(2,1)S(1)}, bf16[2,128,128]{2,1,0:T(8,128)(2,1)S(1)}, u32[]{:S(2)}, u32[]{:S(2)}) collective-permute-start(bf16[2,128,128]{2,1,0:T(8,128)(2,1)S(1)} %pad_maximum_fusion.2), channel_id=1, source_target_pairs={{0,32},{32,0},{16,48},{48,16},{64,96},{96,64},{80,112},{112,80},{1... | collective-permute-start | bytes 196616 | tf_op jit(solution)/shard_map/ppermute | solution.py:40
  130.5 19.4 %collective-permute-done.2 = bf16[4,8,128,128]{3,0,2,1:T(4,128)(2,1)S(1)} collective-permute-done((bf16[4,8,128,128]{3,0,2,1:T(4,128)(2,1)S(1)}, bf16[4,8,128,128]{3,0,2,1:T(4,128)(2,1)S(1)}, u32[]{:S(2)}, u32[]{:S(2)}) %collective-permute-start.2) | collective-permute-done | bytes 1048608 | tf_op jit(solution)/shard_map/ppermute | solution.py:40
  151.9 2.8 %collective-permute-start.4 = (bf16[3,8,128,128]{3,2,1,0:T(8,128)(2,1)S(1)}, bf16[3,8,128,128]{3,2,1,0:T(8,128)(2,1)S(1)}, u32[]{:S(2)}, u32[]{:S(2)}) collective-permute-start(bf16[3,8,128,128]{3,2,1,0:T(8,128)(2,1)S(1)} %copy.54), channel_id=1, source_target_pairs={{0,64},{64,0},{16,80},{80,16},{32,96},{96,32},{48,112},{112,48},{1... | collective-permute-start | bytes 2359304 | tf_op jit(solution)/shard_map/ppermute | solution.py:40
  155.1 2.5 collective-permute-start.5
  158.0 13.6 %collective-permute-done.5 = bf16[2,128,128]{2,1,0:T(8,128)(2,1)S(1)} collective-permute-done((bf16[2,128,128]{2,1,0:T(8,128)(2,1)S(1)}, bf16[2,128,128]{2,1,0:T(8,128)(2,1)S(1)}, u32[]{:S(2)}, u32[]{:S(2)}) %collective-permute-start.5) | collective-permute-done | bytes 65568 | tf_op jit(solution)/shard_map/ppermute | solution.py:40
  174.1 5.4 %collective-permute-start.7 = (bf16[2,128,128]{2,1,0:T(8,128)(2,1)S(1)}, bf16[2,128,128]{2,1,0:T(8,128)(2,1)S(1)}, u32[]{:S(2)}, u32[]{:S(2)}) collective-permute-start(bf16[2,128,128]{2,1,0:T(8,128)(2,1)S(1)} %pad_maximum_fusion.4), channel_id=1, source_target_pairs={{0,128},{128,0},{16,144},{144,16},{32,160},{160,32},{48,176},{176,... | collective-permute-start | bytes 196616 | tf_op jit(solution)/shard_map/ppermute | solution.py:40
  179.5 1.9 collective-permute-start.6
  181.8 26.0 %collective-permute-done.6 = bf16[2,8,128,128]{3,0,2,1:T(2,128)(2,1)S(1)} collective-permute-done((bf16[2,8,128,128]{3,0,2,1:T(2,128)(2,1)S(1)}, bf16[2,8,128,128]{3,0,2,1:T(2,128)(2,1)S(1)}, u32[]{:S(2)}, u32[]{:S(2)}) %collective-permute-start.6) | collective-permute-done | bytes 524320 | tf_op jit(solution)/shard_map/ppermute | solution.py:40
  210.2 8.0 %collective-permute-start.9 = (bf16[2,128,128]{2,1,0:T(8,128)(2,1)S(1)}, bf16[2,128,128]{2,1,0:T(8,128)(2,1)S(1)}, u32[]{:S(2)}, u32[]{:S(2)}) collective-permute-start(bf16[2,128,128]{2,1,0:T(8,128)(2,1)S(1)} %pad_maximum_fusion.5), channel_id=1, source_target_pairs={{0,256},{256,0},{16,272},{272,16},{32,288},{288,32},{48,304},{304,... | collective-permute-start | bytes 196616 | tf_op jit(solution)/shard_map/ppermute | solution.py:40
  218.2 2.1 collective-permute-start.8
  220.7 25.0 %collective-permute-done.8 = bf16[1,8,128,128]{3,0,2,1:T(2,128)(2,1)S(1)} collective-permute-done((bf16[1,8,128,128]{3,0,2,1:T(2,128)(2,1)S(1)}, bf16[1,8,128,128]{3,0,2,1:T(2,128)(2,1)S(1)}, u32[]{:S(2)}, u32[]{:S(2)}) %collective-permute-start.8) | collective-permute-done | bytes 262176 | tf_op jit(solution)/shard_map/ppermute | solution.py:40
  251.5 1.7 fusion.5
  253.2 2.9 %add_convert_fusion = bf16[2,512,512]{2,1,0:T(8,128)(2,1)} fusion(f32[2,512,512]{2,1,0:T(8,128)S(1)} %fusion.5, bf16[2,512,512]{2,1,0:T(8,128)(2,1)S(1)} %copy-done, bf16[2,512,512]{2,1,0:T(8,128)(2,1)} %param.8), kind=kOutput, calls=%fused_computation.4 | convolution fusion | flops 537919488 | bytes 5242880 | tf_op jit(solution)/shard_map/lij,ljk->lik/dot_general | solution.py:162
  (125 shorter events, 31.2 us)
Async XLA Ops:
  6.5 246.7 %copy-start = (bf16[2,512,512]{2,1,0:T(8,128)(2,1)S(1)}, bf16[2,512,512]{2,1,0:T(8,128)(2,1)}, u32[]{:S(2)}) copy-start(bf16[2,512,512]{2,1,0:T(8,128)(2,1)} %param.7) | copy-start | bytes 3145732
  6.5 20.9 %copy-start.2 = (bf16[1,4,2,128,128]{4,3,2,1,0:T(8,128)(2,1)S(1)}, bf16[1,4,2,128,128]{4,3,2,1,0:T(8,128)(2,1)}, u32[]{:S(2)}) copy-start(bf16[1,4,2,128,128]{4,3,2,1,0:T(8,128)(2,1)} %param.12) | copy-start | bytes 786436
  6.5 71.2 %all-gather.3.cloned.1.call-start = ((), (), s32[]{:S(2)}) async-start(), calls=%async_computation.1 | async-start | bytes 4456448 | tf_op jit(solution)/shard_map/all_gather | solution.py:112
  16.0 47.5 %all-to-all-start = ((bf16[16,1,256,128]{3,2,1,0:T(8,128)(2,1)}), bf16[16,1,256,128]{3,2,1,0:T(8,128)(2,1)S(1)}, u32[]{:S(2)}, u32[]{:S(2)}) async-start(bf16[16,1,256,128]{3,2,1,0:T(8,128)(2,1)} %broadcast_in_dim.25), calls=%async_computation | async-start | bytes 2097152 | tf_op jit(solution)/shard_map/all_to_all | solution.py:17
  79.0 2.2 copy-start.1
  81.7 12.2 %collective-permute-start.1 = (bf16[2,128,128]{2,1,0:T(8,128)(2,1)S(1)}, bf16[2,128,128]{2,1,0:T(8,128)(2,1)S(1)}, u32[]{:S(2)}, u32[]{:S(2)}) collective-permute-start(bf16[2,128,128]{2,1,0:T(8,128)(2,1)S(1)} %pad_maximum_fusion.1), channel_id=1, source_target_pairs={{0,16},{16,0},{32,48},{48,32},{64,80},{80,64},{96,112},{112,96},{1... | collective-permute-start | bytes 196616 | tf_op jit(solution)/shard_map/ppermute | solution.py:40
  88.9 31.9 %collective-permute-start = (bf16[5,8,128,128]{3,2,1,0:T(8,128)(2,1)S(1)}, bf16[5,8,128,128]{3,2,1,0:T(8,128)(2,1)S(1)}, u32[]{:S(2)}, u32[]{:S(2)}) collective-permute-start(bf16[5,8,128,128]{3,2,1,0:T(8,128)(2,1)S(1)} %copy.51), channel_id=1, source_target_pairs={{0,16},{16,0},{32,48},{48,32},{64,80},{80,64},{96,112},{112,96},{1... | collective-permute-start | bytes 3932168 | tf_op jit(solution)/shard_map/ppermute | solution.py:40
  122.9 27.0 %collective-permute-start.2 = (bf16[4,8,128,128]{3,0,2,1:T(4,128)(2,1)S(1)}, bf16[4,8,128,128]{3,0,2,1:T(4,128)(2,1)S(1)}, u32[]{:S(2)}, u32[]{:S(2)}) collective-permute-start(bf16[4,8,128,128]{3,0,2,1:T(4,128)(2,1)S(1)} %slice.978), channel_id=1, source_target_pairs={{0,32},{32,0},{16,48},{48,16},{64,96},{96,64},{80,112},{112,80},{1... | collective-permute-start | bytes 3145736 | tf_op jit(solution)/shard_map/ppermute | solution.py:40
  126.9 27.8 %collective-permute-start.3 = (bf16[2,128,128]{2,1,0:T(8,128)(2,1)S(1)}, bf16[2,128,128]{2,1,0:T(8,128)(2,1)S(1)}, u32[]{:S(2)}, u32[]{:S(2)}) collective-permute-start(bf16[2,128,128]{2,1,0:T(8,128)(2,1)S(1)} %pad_maximum_fusion.2), channel_id=1, source_target_pairs={{0,32},{32,0},{16,48},{48,16},{64,96},{96,64},{80,112},{112,80},{1... | collective-permute-start | bytes 196616 | tf_op jit(solution)/shard_map/ppermute | solution.py:40
  151.9 19.7 %collective-permute-start.4 = (bf16[3,8,128,128]{3,2,1,0:T(8,128)(2,1)S(1)}, bf16[3,8,128,128]{3,2,1,0:T(8,128)(2,1)S(1)}, u32[]{:S(2)}, u32[]{:S(2)}) collective-permute-start(bf16[3,8,128,128]{3,2,1,0:T(8,128)(2,1)S(1)} %copy.54), channel_id=1, source_target_pairs={{0,64},{64,0},{16,80},{80,16},{32,96},{96,32},{48,112},{112,48},{1... | collective-permute-start | bytes 2359304 | tf_op jit(solution)/shard_map/ppermute | solution.py:40
  155.1 16.4 %collective-permute-start.5 = (bf16[2,128,128]{2,1,0:T(8,128)(2,1)S(1)}, bf16[2,128,128]{2,1,0:T(8,128)(2,1)S(1)}, u32[]{:S(2)}, u32[]{:S(2)}) collective-permute-start(bf16[2,128,128]{2,1,0:T(8,128)(2,1)S(1)} %pad_maximum_fusion.3), channel_id=1, source_target_pairs={{0,64},{64,0},{16,80},{80,16},{32,96},{96,32},{48,112},{112,48},{1... | collective-permute-start | bytes 196616 | tf_op jit(solution)/shard_map/ppermute | solution.py:40
  174.1 7.6 %collective-permute-start.7 = (bf16[2,128,128]{2,1,0:T(8,128)(2,1)S(1)}, bf16[2,128,128]{2,1,0:T(8,128)(2,1)S(1)}, u32[]{:S(2)}, u32[]{:S(2)}) collective-permute-start(bf16[2,128,128]{2,1,0:T(8,128)(2,1)S(1)} %pad_maximum_fusion.4), channel_id=1, source_target_pairs={{0,128},{128,0},{16,144},{144,16},{32,160},{160,32},{48,176},{176,... | collective-permute-start | bytes 196616 | tf_op jit(solution)/shard_map/ppermute | solution.py:40
  179.5 28.3 %collective-permute-start.6 = (bf16[2,8,128,128]{3,0,2,1:T(2,128)(2,1)S(1)}, bf16[2,8,128,128]{3,0,2,1:T(2,128)(2,1)S(1)}, u32[]{:S(2)}, u32[]{:S(2)}) collective-permute-start(bf16[2,8,128,128]{3,0,2,1:T(2,128)(2,1)S(1)} %slice.998), channel_id=1, source_target_pairs={{0,128},{128,0},{16,144},{144,16},{32,160},{160,32},{48,176},{176,... | collective-permute-start | bytes 1572872 | tf_op jit(solution)/shard_map/ppermute | solution.py:40
  210.2 36.8 %collective-permute-start.9 = (bf16[2,128,128]{2,1,0:T(8,128)(2,1)S(1)}, bf16[2,128,128]{2,1,0:T(8,128)(2,1)S(1)}, u32[]{:S(2)}, u32[]{:S(2)}) collective-permute-start(bf16[2,128,128]{2,1,0:T(8,128)(2,1)S(1)} %pad_maximum_fusion.5), channel_id=1, source_target_pairs={{0,256},{256,0},{16,272},{272,16},{32,288},{288,32},{48,304},{304,... | collective-permute-start | bytes 196616 | tf_op jit(solution)/shard_map/ppermute | solution.py:40
  218.2 27.5 %collective-permute-start.8 = (bf16[1,8,128,128]{3,0,2,1:T(2,128)(2,1)S(1)}, bf16[1,8,128,128]{3,0,2,1:T(2,128)(2,1)S(1)}, u32[]{:S(2)}, u32[]{:S(2)}) collective-permute-start(bf16[1,8,128,128]{3,0,2,1:T(2,128)(2,1)S(1)} %slice.1008), channel_id=1, source_target_pairs={{0,256},{256,0},{16,272},{272,16},{32,288},{288,32},{48,304},{304,... | collective-permute-start | bytes 786440 | tf_op jit(solution)/shard_map/ppermute | solution.py:40
Sparse Core Ops, SparseCore 0:
  10.2 67.4 all-gather.2
where the time goes:
time: 264 us; the launch traced here: 263 us
  waiting for transfers between devices  161 us (61%)
  starting transfers between devices  45.3 us (17%)
  matrix products  23.2 us (9%)
  between operations  14.3 us (5%)
  local copies, waits for them, and re-layouts  9.89 us (4%)
  other arithmetic  9.33 us (4%)
    ppermute x10, waiting for transfers between devices, from_partner(): return lax.ppermute(block, axis, route)  111 us
    all_to_all x1, waiting for transfers between devices, from_everyone(): return lax.all_to_all(copies, axis, split_axis=0, concat_axis=0, tiled=True)  36 us
    ppermute x10, starting transfers between devices, from_partner(): return lax.ppermute(block, axis, route)  35 us
    dot_general x62, matrix products, multiply(): jnp.matmul(first_arg.astype(jnp.float32), second_arg.astype(jnp.float32),...  14.5 us
    all_gather x1, waiting for transfers between devices, shards(): group_gens = lax.all_gather(own_gens[None], 'col', axis=0, tiled=True)  14 us
    all_to_all x1, starting transfers between devices, from_everyone(): return lax.all_to_all(copies, axis, split_axis=0, concat_axis=0, tiled=True)  10.3 us
  transfers between devices with their start and end apart: 12, of which 7 were waited for; matrix products, arithmetic and copies ran while one was open for 7% of the time, Pallas kernels for 0%

commit v1 on v0

v1 whole, which is shorter than its diff:
```python
import jax
import jax.numpy as jnp
from jax import lax
from jax.experimental import pallas as pl
from jax.experimental.pallas import tpu as pltpu
from jax.sharding import PartitionSpec as P

MESH_ID = pl.DeviceIdType.MESH
BF = jnp.bfloat16
F32 = jnp.float32
N_X = 4
N_Y = 8
N_Z = 8
TOP = 9


def flip1(p):
    return p + 1 - 2 * (p % 2)


def flip3(p):
    return p - p % 4 + 3 - p % 4


def halves(v):
    if v.dtype == BF:
        return (v,)
    high = v.astype(BF)
    return high, (v - high.astype(F32)).astype(BF)


def product(a, b, ca, cb):
    a, b = halves(a), halves(b)
    terms = [(i, j) for i in range(len(a)) for j in range(len(b)) if i + j < 2]
    if len(terms) == 1:
        left, right = a[0], b[0]
    else:
        left = jnp.concatenate([a[i] for i, _ in terms], ca)
        right = jnp.concatenate([b[j] for _, j in terms], cb)
    return lax.dot_general(left, right, (((ca,), (cb,)), ((), ())), preferred_element_type=F32)


def mm(a, b):
    return product(a, b, 1, 0)


def mm_t0(a, b):
    return product(a, b, 0, 0)


def mm_t1(a, b):
    return product(a, b, 1, 1)


def kernel(
    da, db, ib, ob, asc, desc, cp, out,
    va, vb, vib, vob, vasc, vdesc, vcp,
    acc, obuf, us, vw, s_f, s_t, r_f, r_t,
    t_pq, t_sw, t_k, low, top, s_fin, r_fin, s_g, r_g,
    ld_sem, st_sem, xs_sem, rf_sem, rt_sem, rpq_sem, rsw_sem, rk_sem,
    hs_sem, low_sem, top_sem, y_sem, tab_sem, fs_sem, fr_sem,
):
    row = lax.axis_index("row")
    col = lax.axis_index("col")
    z, x = row // N_X, row % N_X
    y, core = col // 2, col % 2

    loads = []
    pairs = ((ib, vib), (asc.at[0], vasc), (desc.at[0], vdesc), (cp.at[0], vcp), (ob, vob), (da, va), (db, vb))
    for i, (src, dst) in enumerate(pairs):
        c = pltpu.make_async_copy(src, dst, ld_sem.at[i])
        c.start()
        loads.append(c)

    barrier = pltpu.get_barrier_semaphore()

    def greet_plane(i, carry):
        r = (row + i // 2) % (N_X * N_Z)
        c = y * 2 + (core + i) % 2
        pl.semaphore_signal(barrier, inc=1, device_id=(r, c), device_id_type=MESH_ID)
        return carry

    lax.fori_loop(1, 2 * N_X * N_Z, greet_plane, 0)

    def greet_ring(i, carry):
        c = (col - core + i) % (2 * N_Y)
        pl.semaphore_signal(barrier, inc=1, device_id=(row, c), device_id_type=MESH_ID)
        return carry

    lax.fori_loop(2, 2 * N_Y, greet_ring, 0)

    with jax.named_scope("load"):
        loads[0].wait()
        loads[1].wait()
    leaf = [mm_t0(vib[i, 0], vib[i, 1]) for i in range(2)]
    term = [mm(mm_t0(vasc[i, 0], leaf[i]), vasc[i, 1]) for i in range(2)]
    node = term[0] + term[1]
    lifted = mm(mm_t0(vasc[2, 0], node), vasc[2, 1])
    s_f[1] = node.astype(BF)
    s_t[1] = lifted.astype(BF)

    with jax.named_scope("entry"):
        pl.semaphore_wait(barrier, 2 * N_X * N_Z - 1 + 2 * N_Y - 2)

    def remote(src, dst, ssem, rsem, r, c):
        return pltpu.make_async_remote_copy(
            src_ref=src, dst_ref=dst, send_sem=ssem, recv_sem=rsem,
            device_id=(r, c), device_id_type=MESH_ID,
        )

    def arrived(dst, sem, name="wait"):
        with jax.named_scope(name):
            remote(dst, dst, xs_sem.at[0, 0], sem, row, col).wait_recv()

    def dense(i, r):
        rows = pl.ds(r * 128, 128)
        acc[i, rows, :] = jnp.dot(va[i, rows, :], vb[i], preferred_element_type=F32)

    def side_terms(kl1, kr1):
        near_node = mm(mm(kl1, r_f[1]), kr1)
        for i in range(2):
            kl, kr = (vcp[0, 0], vcp[0, 3]) if i == 0 else (vcp[0, 1], vcp[0, 2])
            g = mm(mm(kl, leaf[1 - i]), kr)
            g = g + mm_t1(mm(vdesc[i, 0], near_node), vdesc[i, 1])
            us[i] = mm(vob[i, 0], mm(vdesc[i, 0], vdesc[2, 0])).astype(BF)
            vw[i] = mm(vob[i, 1], mm(vdesc[i, 1], vdesc[2, 1])).astype(BF)
            acc[i] += mm_t1(mm(vob[i, 0], g.astype(BF)).astype(BF), vob[i, 1])

    def finish(g, left, right):
        arrived(r_f.at[TOP], rf_sem.at[TOP], "wait_f9")
        g = (g + mm(mm(left, r_f[TOP]), right)).astype(BF)
        stores = []
        for i in range(2):
            spread = mm(us[i], g).astype(BF)
            for r in range(2):
                rows = pl.ds(r * 256, 256)
                block = acc[i, rows, :] + mm_t1(spread[r * 256:(r + 1) * 256], vw[i])
                obuf[i, rows, :] = block.astype(BF)
                c = pltpu.make_async_copy(obuf.at[i, rows], out.at[i, rows], st_sem.at[2 * i + r])
                c.start()
                stores.append(c)
        with jax.named_scope("stores"):
            for c in stores:
                c.wait()

    def route(h):
        p = {2: y, 3: y, 4: y, 5: x, 6: x, 7: z, 8: z, 9: z}[h]
        if h in (2, 5, 7):
            return None, flip1(p), None
        if h == 6:
            return None, 3 - p, None
        middle = ((p + 1) // 2) % 2
        if h in (3, 8):
            near = flip3(p)
            return middle == 1, near, flip1(near)
        near = 7 - p
        return middle == 0, near, flip1(near)

    def place(h, p, c):
        if h <= 4:
            return row, p * 2 + c
        if h <= 6:
            return z * N_X + p, y * 2 + c
        return p * N_X + x, y * 2 + c

    def when(cond, f):
        if cond is None:
            f()
        else:
            pl.when(cond)(f)

    def send_f(h, p, c, k):
        r, cc = place(h, p, c)
        return remote(s_f.at[h], r_f.at[h], xs_sem.at[h, k], rf_sem.at[h], r, cc)

    def send_t(h, p, k):
        r, cc = place(h, p, 1)
        return remote(s_t.at[h], r_t.at[h], xs_sem.at[h, k], rt_sem.at[h], r, cc)

    def table_copies(src, h, r, c, side, i):
        return (
            lambda: (remote(src.at[pl.ds(0, 2)], t_pq.at[h], tab_sem.at[0, i], rpq_sem.at[h], r, c),),
            lambda: (remote(src.at[pl.ds(2, 2)], t_sw.at[h], tab_sem.at[1, i], rsw_sem.at[h], r, c),),
            lambda: (
                remote(src.at[4 + side], t_k.at[h, 0], tab_sem.at[2, i], rk_sem.at[h, 0], r, c),
                remote(src.at[7 - side], t_k.at[h, 1], tab_sem.at[3, i], rk_sem.at[h, 1], r, c),
            ),
        )

    @pl.when(core == 1)
    def _():
        me_c = y * 2 + 1
        send = remote(s_f.at[1], r_f.at[1], xs_sem.at[1, 0], rf_sem.at[1], row, me_c - 1)
        send.start()
        loads[2].wait()
        loads[3].wait()

        def hand_over(dst, sems):
            return [
                remote(vasc.at[3], dst.at[pl.ds(0, 2)], hs_sem.at[0], sems.at[0], row, me_c - 1),
                remote(vdesc.at[3], dst.at[pl.ds(2, 2)], hs_sem.at[1], sems.at[1], row, me_c - 1),
                remote(vcp.at[1], dst.at[pl.ds(4, 4)], hs_sem.at[2], sems.at[2], row, me_c - 1),
            ]

        @pl.when(y == 7)
        def _():
            for c in hand_over(top, top_sem):
                c.start()

        @pl.when(y != 7)
        def _():
            for c in hand_over(low, low_sem):
                c.start()

        down = {}

        def compose(h):
            arrived(t_k.at[h, 0], rk_sem.at[h, 0], f"wait_k{h}")
            arrived(t_k.at[h, 1], rk_sem.at[h, 1], f"wait_k{h}")
            left, right = t_k[h, 0], t_k[h, 1]
            if h >= 3:
                arrived(t_sw.at[h - 2], rsw_sem.at[h - 2], f"wait_sw{h - 2}")
                s, w = t_sw[h - 2, 0], t_sw[h - 2, 1]
                if h == 3:
                    down["s"], down["w"] = s, w.T
                else:
                    down["s"] = mm(down["s"], s)
                    down["w"] = mm_t0(w, down["w"])
                left = mm(down["s"], left)
                right = mm(right, down["w"])
            if h == TOP:
                return left, right
            g = mm(mm(left, r_f[h]), right)
            down["g"] = g if h == 2 else down["g"] + g

        def filler(h):
            if h == 2:
                loads[5].wait()
                loads[6].wait()
            if h <= 5:
                dense((h - 2) // 2, (h - 2) % 2 * 2)
                dense((h - 2) // 2, (h - 2) % 2 * 2 + 1)
            if h == 6:
                loads[4].wait()
                arrived(t_k.at[1, 0], rk_sem.at[1, 0])
                arrived(t_k.at[1, 1], rk_sem.at[1, 1])
                side_terms(t_k[1, 0], t_k[1, 1])
                compose(2)
            if h == 7:
                compose(3)
                compose(4)
            if h == 8:
                compose(5)

        arrived(r_f.at[1], rf_sem.at[1])
        arrived(r_t.at[1], rt_sem.at[1], "wait_t1")
        current = lifted + r_t[1].astype(F32)
        for h in range(2, TOP + 1):
            cond, near, far = route(h)
            s_f[h] = current.astype(BF)
            if h == TOP:
                def go():
                    for k, (p, c) in enumerate(((far, 1), (near, 1), (far, 0), (near, 0))):
                        send_f(h, p, c, k).start()
                when(cond, go)
                break
            when(cond, lambda: send_f(h, near if far is None else far, 1, 0).start())
            arrived(t_pq.at[h - 1], rpq_sem.at[h - 1], f"wait_pq{h - 1}")
            term = mm(mm_t0(t_pq[h - 1, 0], current), t_pq[h - 1, 1])
            s_t[h] = term.astype(BF)

            def go():
                if far is not None:
                    send_t(h, far, 2).start()
                send_t(h, near, 1).start()
                if far is not None:
                    send_f(h, near, 1, 3).start()
            when(cond, go)
            with jax.named_scope(f"fill{h}"):
                filler(h)
            arrived(r_t.at[h], rt_sem.at[h], f"wait_t{h}")
            current = term + r_t[h].astype(F32)
            arrived(r_f.at[h], rf_sem.at[h], f"wait_f{h}")
        compose(6)
        compose(7)
        compose(8)
        left, right = compose(9)
        s_fin[0] = left
        s_fin[1] = right
        s_g[...] = down["g"]
        fin = [
            remote(s_fin.at[0], r_fin.at[0], fs_sem.at[0], fr_sem.at[0], row, me_c - 1),
            remote(s_fin.at[1], r_fin.at[1], fs_sem.at[1], fr_sem.at[1], row, me_c - 1),
            remote(s_g, r_g, fs_sem.at[2], fr_sem.at[2], row, me_c - 1),
        ]
        for c in fin:
            c.start()
        finish(down["g"], left, right)
        send.wait_send()
        for c in fin + hand_over(low, low_sem):
            c.wait_send()
        for h in range(2, TOP + 1):
            cond, near, far = route(h)

            def drain():
                if h == TOP:
                    for k, (p, c) in enumerate(((far, 1), (near, 1), (far, 0), (near, 0))):
                        send_f(h, p, c, k).wait_send()
                    return
                send_f(h, near if far is None else far, 1, 0).wait_send()
                if far is not None:
                    send_t(h, far, 2).wait_send()
                send_t(h, near, 1).wait_send()
                if far is not None:
                    send_f(h, near, 1, 3).wait_send()
            when(cond, drain)

    @pl.when(core == 0)
    def _():
        peer = y * 2 + 1
        mine = [
            remote(s_t.at[1], r_t.at[1], xs_sem.at[1, 0], rt_sem.at[1], row, peer),
            remote(s_f.at[1], r_f.at[1], xs_sem.at[1, 1], rf_sem.at[1], row, peer),
            remote(vasc.at[3], t_pq.at[1], xs_sem.at[2, 0], rpq_sem.at[1], row, peer),
        ]
        for c in mine:
            c.start()
        loads[2].wait()
        loads[3].wait()
        more = [
            remote(vdesc.at[3], t_sw.at[1], xs_sem.at[2, 1], rsw_sem.at[1], row, peer),
            remote(vcp.at[1, 1], t_k.at[1, 0], xs_sem.at[3, 0], rk_sem.at[1, 0], row, peer),
            remote(vcp.at[1, 2], t_k.at[1, 1], xs_sem.at[3, 1], rk_sem.at[1, 1], row, peer),
        ]
        for c in more:
            c.start()
        mine += more

        def low_copies(h):
            size = 2 ** (h - 1)
            base = y - y % size
            for i in range(size):
                yield table_copies(low, h, row, (base + i) * 2 + 1, i // (size // 2), i)

        @pl.when(y != 7)
        def _():
            arrived(low.at[pl.ds(0, 2)], low_sem.at[0], "wait_low")
            for h in (2, 3, 4):
                @pl.when(y % 2 ** (h - 1) == 2 ** (h - 2) - 1)
                def _():
                    for c in low_copies(h):
                        c[0]()[0].start()
            arrived(low.at[pl.ds(2, 2)], low_sem.at[1])
            arrived(low.at[pl.ds(4, 4)], low_sem.at[2])
            for h in (2, 3, 4):
                @pl.when(y % 2 ** (h - 1) == 2 ** (h - 2) - 1)
                def _():
                    for k in (2, 1):
                        for c in low_copies(h):
                            for d in c[k]():
                                d.start()

        parts = (pl.ds(0, 2), pl.ds(2, 2), pl.ds(4, 4))

        def ring_copy(k, j):
            return remote(
                top.at[parts[k]], top.at[parts[k]], y_sem.at[k, j], top_sem.at[k], row, j * 2
            )

        def owns(h):
            return row % 2 ** (h - 4) == 2 ** (h - 5) - 1

        def plane_copy(h, i):
            size = 2 ** (h - 4)
            return table_copies(top, h, row - row % size + i, peer, i // (size // 2), i)

        def upper(k):
            heights = (5, 6, 7, 8, 9) if k == 2 else (5, 6, 7)
            at_top = row % 32 != 31 if k == 2 else row % 8 != 7

            @pl.when(at_top)
            def _():
                arrived(top.at[parts[k]], top_sem.at[k], f"wait_top{k}")

                @pl.when(y == 7)
                def _():
                    for j in (3, 4, 2, 5, 1, 0, 6):
                        ring_copy(k, j).start()

                for h in heights:
                    @pl.when(owns(h))
                    def _():
                        def body(i, carry):
                            for d in plane_copy(h, i)[k]():
                                d.start()
                            return carry
                        lax.fori_loop(0, 2 ** (h - 4), body, 0)

        def local_work():
            loads[5].wait()
            loads[6].wait()
            for i in range(2):
                for r in range(4):
                    dense(i, r)
            loads[4].wait()
            arrived(r_f.at[1], rf_sem.at[1])
            side_terms(vcp[1, 0], vcp[1, 3])

        @pl.when(y == 7)
        def _():
            upper(0)

        with jax.named_scope("local"):
            local_work()

        @pl.when(y != 7)
        def _():
            upper(0)

        upper(2)
        upper(1)

        arrived(r_fin.at[0], fr_sem.at[0])
        arrived(r_fin.at[1], fr_sem.at[1])
        arrived(r_g, fr_sem.at[2], "wait_g")
        finish(r_g[...], r_fin[0], r_fin[1])

        for c in mine:
            c.wait_send()

        @pl.when(y != 7)
        def _():
            for h in (2, 3, 4):
                @pl.when(y % 2 ** (h - 1) == 2 ** (h - 2) - 1)
                def _():
                    for c in low_copies(h):
                        for k in range(3):
                            for d in c[k]():
                                d.wait_send()

        for k in range(3):
            heights = (5, 6, 7, 8, 9) if k == 2 else (5, 6, 7)
            at_top = row % 32 != 31 if k == 2 else row % 8 != 7

            @pl.when(at_top)
            def _():
                @pl.when(y == 7)
                def _():
                    for j in range(7):
                        ring_copy(k, j).wait_send()

                for h in heights:
                    @pl.when(owns(h))
                    def _():
                        def body(i, carry):
                            for d in plane_copy(h, i)[k]():
                                d.wait_send()
                            return carry
                        lax.fori_loop(0, 2 ** (h - 4), body, 0)

            @pl.when(jnp.logical_not(at_top))
            def _():
                @pl.when(y == 7)
                def _():
                    arrived(top.at[parts[k]], top_sem.at[k])


def shards(dense_a, dense_b, inner, outer, ascent, descent, couplings):
    any_spec = pl.BlockSpec(memory_space=pl.ANY)
    dma = pltpu.SemaphoreType.DMA
    tile = (128, 128)
    return pl.pallas_call(
        kernel,
        out_shape=jax.ShapeDtypeStruct((2, 512, 512), BF),
        in_specs=[any_spec] * 7,
        out_specs=any_spec,
        scratch_shapes=[
            pltpu.VMEM((2, 512, 512), BF),
            pltpu.VMEM((2, 512, 512), BF),
            pltpu.VMEM((2, 2, 512, 128), BF),
            pltpu.VMEM((2, 2, 512, 128), BF),
            pltpu.VMEM((4, 2, *tile), BF),
            pltpu.VMEM((4, 2, *tile), BF),
            pltpu.VMEM((2, 4, *tile), BF),
            pltpu.VMEM((2, 512, 512), F32),
            pltpu.VMEM((2, 512, 512), BF),
            pltpu.VMEM((2, 512, 128), BF),
            pltpu.VMEM((2, 512, 128), BF),
            pltpu.VMEM((10, *tile), BF),
            pltpu.VMEM((10, *tile), BF),
            pltpu.VMEM((10, *tile), BF),
            pltpu.VMEM((10, *tile), BF),
            pltpu.VMEM((8, 2, *tile), BF),
            pltpu.VMEM((8, 2, *tile), BF),
            pltpu.VMEM((10, 2, *tile), BF),
            pltpu.VMEM((8, *tile), BF),
            pltpu.VMEM((8, *tile), BF),
            pltpu.VMEM((2, *tile), F32),
            pltpu.VMEM((2, *tile), F32),
            pltpu.VMEM(tile, F32),
            pltpu.VMEM(tile, F32),
            dma((7,)),
            dma((4,)),
            dma((10, 4)),
            dma((10,)),
            dma((10,)),
            dma((8,)),
            dma((8,)),
            dma((10, 2)),
            dma((3,)),
            dma((3,)),
            dma((3,)),
            dma((3, 7)),
            dma((4, 32)),
            dma((3,)),
            dma((3,)),
        ],
        compiler_params=pltpu.CompilerParams(collective_id=0, has_side_effects=True),
        name="tree",
    )(dense_a, dense_b, inner, outer, ascent, descent, couplings)


def solution(mesh):
    placed = (
        P(("row", "col"), None, None),
        P(("row", "col"), None, None),
        P(("row", "col"), None, None, None),
        P(("row", "col"), None, None, None),
        P(("row", "col"), None, None, None, None),
        P(("row", "col"), None, None, None, None),
        P(("row", "col"), None, None, None, None),
    )
    return jax.shard_map(
        shards, mesh=mesh, in_specs=placed, out_specs=P(("row", "col"), None, None), check_vma=False
    )
```

time: 264 us -> 51.9 us (0.20)
  the two profiles are of different devices: /device:TPU:1 before, /device:TPU:6 now
where the time goes in v1:
time: 51.9 us; the launch traced here: 51.8 us
  Pallas kernels  49.5 us (95%)
  local copies, waits for them, and re-layouts  2.26 us (4%)
    pallas_call x1, Pallas kernels, shards(): pl.pallas_call(kernel, out_shape=jax.ShapeDtypeStruct((2, 512, 512), BF),...  49.5 us
    unnamed x1, local copies, waits for them, and re-layouts  2.26 us

profile of v1, /device:TPU:6, one launch (start us, length us, event | category | flops | bytes accessed | tf_op | source)
XLA Modules:
  0.0 51.8 jit_solution(5121330489898316385)
XLA Ops:
  0.0 49.5 %tree.1 = bf16[2,512,512]{2,1,0:T(8,128)(2,1)} custom-call(bf16[2,512,512]{2,1,0:T(8,128)(2,1)} %da.1, bf16[2,512,512]{2,1,0:T(8,128)(2,1)} %db.1, bf16[2,2,512,128]{3,2,1,0:T(8,128)(2,1)} %ib.1, bf16[2,2,512,128]{3,2,1,0:T(8,128)(2,1)} %ob.1, bf16[1,4,2,128,128]{4,3,2,1,0:T(8,128)(2,1)} %asc.1, bf16[1,4,2,128,128]{4,3,2,1,0:T(8,128)(2,1)} %desc.1, ...), custom_call_target="tpu_custom_call" | custom-call | tf_op jit(solution)/shard_map/tree/pallas_call | solution.py:472
  49.5 2.3 %copy.9 = bf16[2,512,512]{2,1,0:T(8,128)(2,1)} copy(bf16[2,512,512]{2,1,0:T(8,128)(2,1)} %tree.1) | data formatting | bytes 2097152

commit v2 on v1

v2 whole, which is shorter than its diff:
```python
import jax
import jax.numpy as jnp
from jax import lax
from jax.experimental import pallas as pl
from jax.experimental.pallas import tpu as pltpu
from jax.sharding import PartitionSpec as P

MESH_ID = pl.DeviceIdType.MESH
BF = jnp.bfloat16
F32 = jnp.float32
N_X = 4
N_Y = 8
N_Z = 8
TOP = 9


def flip1(p):
    return p + 1 - 2 * (p % 2)


def flip3(p):
    return p - p % 4 + 3 - p % 4


def halves(v):
    if v.dtype == BF:
        return (v,)
    high = v.astype(BF)
    return high, (v - high.astype(F32)).astype(BF)


def product(a, b, ca, cb):
    a, b = halves(a), halves(b)
    terms = [(i, j) for i in range(len(a)) for j in range(len(b)) if i + j < 2]
    if len(terms) == 1:
        left, right = a[0], b[0]
    else:
        left = jnp.concatenate([a[i] for i, _ in terms], ca)
        right = jnp.concatenate([b[j] for _, j in terms], cb)
    return lax.dot_general(left, right, (((ca,), (cb,)), ((), ())), preferred_element_type=F32)


def mm(a, b):
    return product(a, b, 1, 0)


def mm_t0(a, b):
    return product(a, b, 0, 0)


def mm_t1(a, b):
    return product(a, b, 1, 1)


def kernel(
    da, db, ib, ob, asc, desc, cp, out,
    va, vb, vib, vob, vasc, vdesc, vcp,
    acc, obuf, us, vw, s_f, s_t, r_f, r_t,
    t_pq, t_sw, t_k, low, top, s_fin, r_fin,
    ld_sem, st_sem, xs_sem, rf_sem, rt_sem, rpq_sem, rsw_sem, rk_sem,
    hs_sem, low_sem, top_sem, y_sem, tab_sem, lows_sem, own_sem, fs_sem, fr_sem, go_sem,
):
    row = lax.axis_index("row")
    col = lax.axis_index("col")
    z, x = row // N_X, row % N_X
    y, core = col // 2, col % 2

    def position(h):
        return y if h <= 4 else x if h <= 6 else z

    def route(h):
        p = position(h)
        if h in (2, 5, 7):
            return None, flip1(p), None
        if h == 6:
            return None, 3 - p, None
        middle = ((p + 1) // 2) % 2
        if h in (3, 8):
            near = flip3(p)
            return middle == 1, near, flip1(near)
        near = 7 - p
        return middle == 0, near, flip1(near)

    def sender(h, p):
        if h in (2, 5, 7):
            return flip1(p)
        if h == 6:
            return 3 - p
        middle = ((p + 1) // 2) % 2
        if h in (3, 8):
            return jnp.where(middle == 1, flip3(p), flip1(flip3(p)))
        return jnp.where(middle == 0, 7 - p, flip1(7 - p))

    def place(h, p, c):
        if h <= 4:
            return row, p * 2 + c
        if h <= 6:
            return z * N_X + p, y * 2 + c
        return p * N_X + x, y * 2 + c

    loads = []
    pairs = ((ib, vib), (asc.at[0], vasc), (desc.at[0], vdesc), (cp.at[0], vcp), (ob, vob), (da, va), (db, vb))
    for i, (src, dst) in enumerate(pairs):
        c = pltpu.make_async_copy(src, dst, ld_sem.at[i])
        c.start()
        loads.append(c)

    barrier = pltpu.get_barrier_semaphore()

    def greet(r, c):
        pl.semaphore_signal(barrier, inc=1, device_id=(r, c), device_id_type=MESH_ID)

    middle_y, middle_z = ((y + 1) // 2) % 2, ((z + 1) // 2) % 2
    low_size = jnp.where(y % 2 == 0, 2, jnp.where(y % 4 == 1, 4, 8))
    top_size = jnp.where(x % 2 == 0, 2, jnp.where(x == 1, 4, jnp.where(z % 2 == 0, 8, jnp.where(z % 4 == 1, 16, 32))))
    top_size = jnp.where(row == N_X * N_Z - 1, 0, top_size)

    @pl.when(core == 0)
    def _():
        greet(row, col + 1)
        greet(sender(TOP, z) * N_X + x, y * 2 + 1)

        @pl.when(y != 7)
        def _():
            greet(row, 14)

    @pl.when(core == 1)
    def _():
        greet(row, col - 1)
        for h in (2, 3, 4):
            greet(row, (y - y % 2 ** (h - 1) + 2 ** (h - 2) - 1) * 2)
        for h in range(2, TOP + 1):
            greet(*place(h, sender(h, position(h)), 1))
        for h in range(5, TOP + 1):
            greet(row - row % 2 ** (h - 4) + 2 ** (h - 5) - 1, y * 2)

    receivers = jnp.where(
        core == 0,
        1 + jnp.where(y == 7, 7, low_size) + top_size,
        5 + 2 * middle_y + 2 * (1 - middle_y) + 2 * middle_z + 4 * (1 - middle_z),
    )

    with jax.named_scope("load"):
        loads[0].wait()
        loads[1].wait()
    leaf = [mm_t0(vib[i, 0], vib[i, 1]) for i in range(2)]
    term = [mm(mm_t0(vasc[i, 0], leaf[i]), vasc[i, 1]) for i in range(2)]
    node = term[0] + term[1]
    lifted = mm(mm_t0(vasc[2, 0], node), vasc[2, 1])
    s_f[1] = node.astype(BF)
    s_t[1] = lifted.astype(BF)

    with jax.named_scope("entry"):
        pl.semaphore_wait(barrier, receivers)

    def remote(src, dst, ssem, rsem, r, c):
        return pltpu.make_async_remote_copy(
            src_ref=src, dst_ref=dst, send_sem=ssem, recv_sem=rsem,
            device_id=(r, c), device_id_type=MESH_ID,
        )

    def arrived(dst, sem, name="wait"):
        with jax.named_scope(name):
            remote(dst, dst, xs_sem.at[0], sem, row, col).wait_recv()

    def sent(src, sem):
        remote(src, src, sem, rf_sem.at[0], row, col).wait_send()

    def dense(i, r):
        rows = pl.ds(r * 128, 128)
        acc[i, rows, :] = jnp.dot(va[i, rows, :], vb[i], preferred_element_type=F32)

    def side_terms(i, kl1, kr1):
        near_node = mm(mm(kl1, r_f[1]), kr1)
        if True:
            kl, kr = (vcp[0, 0], vcp[0, 3]) if i == 0 else (vcp[0, 1], vcp[0, 2])
            g = mm(mm(kl, leaf[1 - i]), kr)
            g = g + mm_t1(mm(vdesc[i, 0], near_node), vdesc[i, 1])
            us[i] = mm(vob[i, 0], mm(vdesc[i, 0], vdesc[2, 0])).astype(BF)
            vw[i] = mm(vob[i, 1], mm(vdesc[i, 1], vdesc[2, 1])).astype(BF)
            acc[i] += mm_t1(mm(vob[i, 0], g.astype(BF)).astype(BF), vob[i, 1])

    def finish(g, left, right):
        arrived(r_f.at[TOP], rf_sem.at[TOP], "wait_f9")
        g = (g + mm(mm(left, r_f[TOP]), right)).astype(BF)
        for i in range(2):
            spread = mm(us[i], g).astype(BF)
            for r in range(2):
                rows = pl.ds(r * 256, 256)
                block = acc[i, rows, :] + mm_t1(spread[r * 256:(r + 1) * 256], vw[i])
                obuf[i, rows, :] = block.astype(BF)
                c = pltpu.make_async_copy(obuf.at[i, rows], out.at[i, rows], st_sem)
                c.start()
        with jax.named_scope("stores"):
            pltpu.make_async_copy(obuf, out, st_sem).wait()

    def when(cond, f):
        if cond is None:
            f()
        else:
            pl.when(cond)(f)

    def send_f(h, p, c):
        r, cc = place(h, p, c)
        return remote(s_f.at[h], r_f.at[h], xs_sem.at[h], rf_sem.at[h], r, cc)

    def send_t(h, p):
        r, cc = place(h, p, 1)
        return remote(s_t.at[h], r_t.at[h], xs_sem.at[h], rt_sem.at[h], r, cc)

    def table_copies(src, sem, h, r, c, side):
        return (
            lambda: (remote(src.at[pl.ds(0, 2)], t_pq.at[h], sem.at[0], rpq_sem.at[h], r, c),),
            lambda: (remote(src.at[pl.ds(2, 2)], t_sw.at[h], sem.at[1], rsw_sem.at[h], r, c),),
            lambda: (
                remote(src.at[4 + side], t_k.at[h, 0], sem.at[2], rk_sem.at[h], r, c),
                remote(src.at[7 - side], t_k.at[h, 1], sem.at[2], rk_sem.at[h], r, c),
            ),
        )

    @pl.when(core == 1)
    def _():
        me_c = y * 2 + 1
        send = remote(s_f.at[1], r_f.at[1], xs_sem.at[1], rf_sem.at[1], row, me_c - 1)
        send.start()
        loads[2].wait()
        loads[3].wait()

        def hand_over(dst, sems):
            return [
                remote(vasc.at[3], dst.at[pl.ds(0, 2)], hs_sem.at[0], sems.at[0], row, me_c - 1),
                remote(vdesc.at[3], dst.at[pl.ds(2, 2)], hs_sem.at[0], sems.at[1], row, me_c - 1),
                remote(vcp.at[1], dst.at[pl.ds(4, 4)], hs_sem.at[0], sems.at[2], row, me_c - 1),
            ]

        @pl.when(y == 7)
        def _():
            for c in hand_over(top, top_sem):
                c.start()

        @pl.when(y != 7)
        def _():
            for c in hand_over(low, low_sem):
                c.start()

        down = {}

        def compose(h):
            arrived(t_k.at[h], rk_sem.at[h], f"wait_k{h}")
            left, right = t_k[h, 0], t_k[h, 1]
            if h >= 3:
                arrived(t_sw.at[h - 2], rsw_sem.at[h - 2], f"wait_sw{h - 2}")
                s, w = t_sw[h - 2, 0], t_sw[h - 2, 1]
                if h == 3:
                    down["s"], down["w"] = s, w.T
                else:
                    down["s"] = mm(down["s"], s)
                    down["w"] = mm_t0(w, down["w"])
                left = mm(down["s"], left)
                right = mm(right, down["w"])
            if h == TOP:
                return left, right
            g = mm(mm(left, r_f[h]), right)
            down["g"] = g if h == 2 else down["g"] + g

        def filler(h):
            if h == 2:
                loads[5].wait()
                loads[6].wait()
                for r in range(4):
                    dense(0, r)
            if h == 3:
                for r in range(4):
                    dense(1, r)
                arrived(t_k.at[1], rk_sem.at[1])
                loads[4].wait()
                side_terms(0, t_k[1, 0], t_k[1, 1])
            if h == 4:
                side_terms(1, t_k[1, 0], t_k[1, 1])
            if h == 7:
                compose(2)
                compose(3)
            if h == 8:
                compose(4)
                compose(5)
                compose(6)

        arrived(r_f.at[1], rf_sem.at[1])
        arrived(r_t.at[1], rt_sem.at[1], "wait_t1")
        current = lifted + r_t[1].astype(F32)
        for h in range(2, TOP + 1):
            cond, near, far = route(h)
            s_f[h] = current.astype(BF)
            if h == TOP:
                def go():
                    for p, c in ((far, 1), (near, 1), (far, 0), (near, 0)):
                        send_f(h, p, c).start()
                when(cond, go)
                break
            when(cond, lambda: send_f(h, near if far is None else far, 1).start())
            arrived(t_pq.at[h - 1], rpq_sem.at[h - 1], f"wait_pq{h - 1}")
            term = mm(mm_t0(t_pq[h - 1, 0], current), t_pq[h - 1, 1])
            s_t[h] = term.astype(BF)

            def go():
                if far is not None:
                    send_t(h, far).start()
                send_t(h, near).start()
                if far is not None:
                    send_f(h, near, 1).start()
            when(cond, go)
            with jax.named_scope(f"fill{h}"):
                filler(h)
            arrived(r_t.at[h], rt_sem.at[h], f"wait_t{h}")
            current = term + r_t[h].astype(F32)
            if h == 4:
                pl.semaphore_signal(go_sem, inc=1, device_id=(row, me_c - 1), device_id_type=MESH_ID)
            arrived(r_f.at[h], rf_sem.at[h], f"wait_f{h}")
        compose(7)
        compose(8)
        left, right = compose(9)
        s_fin[0] = left
        s_fin[1] = right
        s_fin[2] = down["g"]
        fin = remote(s_fin, r_fin, fs_sem, fr_sem, row, me_c - 1)
        fin.start()
        finish(down["g"], left, right)
        send.wait_send()
        fin.wait_send()
        sent(low, hs_sem.at[0])
        for h in range(2, TOP + 1):
            cond, near, far = route(h)
            count = 2 if far is None else 4
            when(cond, lambda: sent(s_f.at[pl.ds(0, count)], xs_sem.at[h]))

    @pl.when(core == 0)
    def _():
        peer = y * 2 + 1
        mine = [
            remote(s_t.at[1], r_t.at[1], own_sem.at[0], rt_sem.at[1], row, peer),
            remote(s_f.at[1], r_f.at[1], own_sem.at[1], rf_sem.at[1], row, peer),
            remote(vasc.at[3], t_pq.at[1], own_sem.at[2], rpq_sem.at[1], row, peer),
        ]
        for c in mine:
            c.start()
        loads[2].wait()
        loads[3].wait()
        more = [
            remote(vdesc.at[3], t_sw.at[1], own_sem.at[3], rsw_sem.at[1], row, peer),
            remote(vcp.at[1, 1], t_k.at[1, 0], own_sem.at[4], rk_sem.at[1], row, peer),
            remote(vcp.at[1, 2], t_k.at[1, 1], own_sem.at[5], rk_sem.at[1], row, peer),
        ]
        for c in more:
            c.start()
        mine += more

        def low_copies(h):
            size = 2 ** (h - 1)
            base = y - y % size
            for i in range(size):
                yield table_copies(low, lows_sem, h, row, (base + i) * 2 + 1, i // (size // 2))

        @pl.when(y != 7)
        def _():
            arrived(low.at[pl.ds(0, 2)], low_sem.at[0], "wait_low")
            for h in (2, 3, 4):
                @pl.when(y % 2 ** (h - 1) == 2 ** (h - 2) - 1)
                def _():
                    for c in low_copies(h):
                        c[0]()[0].start()

        def low_rest():
            arrived(low.at[pl.ds(2, 2)], low_sem.at[1])
            arrived(low.at[pl.ds(4, 4)], low_sem.at[2])
            for h in (2, 3, 4):
                @pl.when(y % 2 ** (h - 1) == 2 ** (h - 2) - 1)
                def _():
                    for k in (2, 1):
                        for c in low_copies(h):
                            for d in c[k]():
                                d.start()

        parts = (pl.ds(0, 2), pl.ds(2, 2), pl.ds(4, 4))

        def ring_copy(k, j):
            return remote(
                top.at[parts[k]], top.at[parts[k]], y_sem.at[k], top_sem.at[k], row, j * 2
            )

        def owns(h):
            return row % 2 ** (h - 4) == 2 ** (h - 5) - 1

        def plane_copy(h, i):
            size = 2 ** (h - 4)
            return table_copies(top, tab_sem, h, row - row % size + i, peer, i // (size // 2))

        def upper(k, heights):
            here = (row % 8 != 7) if heights[0] == 5 else (row % 8 == 7) & (row != 31)

            @pl.when(here)
            def _():
                arrived(top.at[parts[k]], top_sem.at[k], f"wait_top{k}")

                @pl.when(y == 7)
                def _():
                    for j in (3, 4, 2, 5, 1, 0, 6):
                        ring_copy(k, j).start()

                for h in heights:
                    @pl.when(owns(h))
                    def _():
                        def body(i, carry):
                            for d in plane_copy(h, i)[k]():
                                d.start()
                            return carry
                        lax.fori_loop(0, 2 ** (h - 4), body, 0)

        def first_tables():
            upper(0, (5, 6, 7))
            upper(2, (8, 9))

        def local_work():
            loads[5].wait()
            loads[6].wait()
            for i in range(2):
                for r in range(4):
                    dense(i, r)
            loads[4].wait()
            arrived(r_f.at[1], rf_sem.at[1])
            for i in range(2):
                side_terms(i, vcp[1, 0], vcp[1, 3])

        @pl.when(y == 7)
        def _():
            first_tables()

        with jax.named_scope("local"):
            local_work()

        @pl.when(y != 7)
        def _():
            first_tables()

        with jax.named_scope("go"):
            pl.semaphore_wait(go_sem, 1)
        upper(2, (5, 6, 7))
        pl.when(y != 7)(low_rest)
        upper(1, (5, 6, 7))

        arrived(r_fin, fr_sem, "wait_fin")
        finish(r_fin[2], r_fin[0], r_fin[1])

        for c in mine:
            c.wait_send()

        @pl.when(y != 7)
        def _():
            for h in (2, 3, 4):
                @pl.when(y % 2 ** (h - 1) == 2 ** (h - 2) - 1)
                def _():
                    for k in range(3):
                        sent(acc.at[0, pl.ds(0, 32 * 2 ** (h - 1))], lows_sem.at[k])

        def drained(k, heights):
            here = (row % 8 != 7) if heights[0] == 5 else (row % 8 == 7) & (row != 31)

            @pl.when(here)
            def _():
                @pl.when(y == 7)
                def _():
                    sent(acc.at[0, pl.ds(0, 32 * 7 * (2 if k == 2 else 1))], y_sem.at[k])

                for h in heights:
                    @pl.when(owns(h))
                    def _():
                        if h == 9:
                            sent(acc, tab_sem.at[k])
                        else:
                            sent(acc.at[0, pl.ds(0, 32 * 2 ** (h - 4))], tab_sem.at[k])

        drained(0, (5, 6, 7))
        drained(1, (5, 6, 7))
        drained(2, (5, 6, 7))
        drained(2, (8, 9))

        @pl.when((y == 7) & (row % 8 == 7))
        def _():
            arrived(top.at[parts[0]], top_sem.at[0])
            arrived(top.at[parts[1]], top_sem.at[1])

        @pl.when((y == 7) & (row == 31))
        def _():
            arrived(top.at[parts[2]], top_sem.at[2])


def shards(dense_a, dense_b, inner, outer, ascent, descent, couplings):
    any_spec = pl.BlockSpec(memory_space=pl.ANY)
    dma = pltpu.SemaphoreType.DMA
    tile = (128, 128)
    return pl.pallas_call(
        kernel,
        out_shape=jax.ShapeDtypeStruct((2, 512, 512), BF),
        in_specs=[any_spec] * 7,
        out_specs=any_spec,
        scratch_shapes=[
            pltpu.VMEM((2, 512, 512), BF),
            pltpu.VMEM((2, 512, 512), BF),
            pltpu.VMEM((2, 2, 512, 128), BF),
            pltpu.VMEM((2, 2, 512, 128), BF),
            pltpu.VMEM((4, 2, *tile), BF),
            pltpu.VMEM((4, 2, *tile), BF),
            pltpu.VMEM((2, 4, *tile), BF),
            pltpu.VMEM((2, 512, 512), F32),
            pltpu.VMEM((2, 512, 512), BF),
            pltpu.VMEM((2, 512, 128), BF),
            pltpu.VMEM((2, 512, 128), BF),
            pltpu.VMEM((10, *tile), BF),
            pltpu.VMEM((10, *tile), BF),
            pltpu.VMEM((10, *tile), BF),
            pltpu.VMEM((10, *tile), BF),
            pltpu.VMEM((8, 2, *tile), BF),
            pltpu.VMEM((8, 2, *tile), BF),
            pltpu.VMEM((10, 2, *tile), BF),
            pltpu.VMEM((8, *tile), BF),
            pltpu.VMEM((8, *tile), BF),
            pltpu.VMEM((3, *tile), F32),
            pltpu.VMEM((3, *tile), F32),
            dma((7,)),
            dma,
            dma((10,)),
            dma((10,)),
            dma((10,)),
            dma((8,)),
            dma((8,)),
            dma((10,)),
            dma((1,)),
            dma((3,)),
            dma((3,)),
            dma((3,)),
            dma((3,)),
            dma((3,)),
            dma((6,)),
            dma,
            dma,
            pltpu.SemaphoreType.REGULAR,
        ],
        compiler_params=pltpu.CompilerParams(collective_id=0, has_side_effects=True),
        name="tree",
    )(dense_a, dense_b, inner, outer, ascent, descent, couplings)


def solution(mesh):
    placed = (
        P(("row", "col"), None, None),
        P(("row", "col"), None, None),
        P(("row", "col"), None, None, None),
        P(("row", "col"), None, None, None),
        P(("row", "col"), None, None, None, None),
        P(("row", "col"), None, None, None, None),
        P(("row", "col"), None, None, None, None),
    )
    return jax.shard_map(
        shards, mesh=mesh, in_specs=placed, out_specs=P(("row", "col"), None, None), check_vma=False
    )
```

time: 51.9 us -> 47.2 us (0.909)
  the two profiles are of different devices: /device:TPU:6 before, /device:TPU:58 now
where the time goes in v2:
time: 47.2 us; the launch traced here: 47.1 us
  Pallas kernels  44.8 us (95%)
  local copies, waits for them, and re-layouts  2.26 us (5%)
    pallas_call x1, Pallas kernels, shards(): pl.pallas_call(kernel, out_shape=jax.ShapeDtypeStruct((2, 512, 512), BF),...  44.8 us
    unnamed x1, local copies, waits for them, and re-layouts  2.26 us

profile of v2, /device:TPU:58, one launch (start us, length us, event | category | flops | bytes accessed | tf_op | source)
XLA Modules:
  0.0 47.1 jit_solution(6040560982726114679)
XLA Ops:
  0.0 44.8 %tree.1 = bf16[2,512,512]{2,1,0:T(8,128)(2,1)} custom-call(bf16[2,512,512]{2,1,0:T(8,128)(2,1)} %da.1, bf16[2,512,512]{2,1,0:T(8,128)(2,1)} %db.1, bf16[2,2,512,128]{3,2,1,0:T(8,128)(2,1)} %ib.1, bf16[2,2,512,128]{3,2,1,0:T(8,128)(2,1)} %ob.1, bf16[1,4,2,128,128]{4,3,2,1,0:T(8,128)(2,1)} %asc.1, bf16[1,4,2,128,128]{4,3,2,1,0:T(8,128)(2,1)} %desc.1, ...), custom_call_target="tpu_custom_call" | custom-call | tf_op jit(solution)/shard_map/tree/pallas_call | solution.py:500
  44.8 2.3 %copy.9 = bf16[2,512,512]{2,1,0:T(8,128)(2,1)} copy(bf16[2,512,512]{2,1,0:T(8,128)(2,1)} %tree.1) | data formatting | bytes 2097152

commit v3 on v2

--- a/solution.py
+++ b/solution.py
@@ -11,6 +11,7 @@
 N_X = 4
 N_Y = 8
 N_Z = 8
+GO = 3
 TOP = 9
 
 
@@ -56,9 +57,9 @@
     da, db, ib, ob, asc, desc, cp, out,
     va, vb, vib, vob, vasc, vdesc, vcp,
     acc, obuf, us, vw, s_f, s_t, r_f, r_t,
-    t_pq, t_sw, t_k, low, top, s_fin, r_fin,
+    t_pq, t_sw, t_k, low, top, mid, s_fin, r_fin,
     ld_sem, st_sem, xs_sem, rf_sem, rt_sem, rpq_sem, rsw_sem, rk_sem,
-    hs_sem, low_sem, top_sem, y_sem, tab_sem, lows_sem, own_sem, fs_sem, fr_sem, go_sem,
+    hs_sem, low_sem, top_sem, mid_sem, y_sem, tab_sem, lows_sem, own_sem, fs_sem, fr_sem, go_sem, rdy_sem, mrdy_sem, hd_sem,
 ):
     row = lax.axis_index("row")
     col = lax.axis_index("col")
@@ -98,6 +99,10 @@
             return z * N_X + p, y * 2 + c
         return p * N_X + x, y * 2 + c
 
+    def keeper(h):
+        size = 2 ** (h - 6)
+        return z - z % size + size // 2 - 1
+
     loads = []
     pairs = ((ib, vib), (asc.at[0], vasc), (desc.at[0], vdesc), (cp.at[0], vcp), (ob, vob), (da, va), (db, vb))
     for i, (src, dst) in enumerate(pairs):
@@ -112,32 +117,52 @@
 
     middle_y, middle_z = ((y + 1) // 2) % 2, ((z + 1) // 2) % 2
     low_size = jnp.where(y % 2 == 0, 2, jnp.where(y % 4 == 1, 4, 8))
-    top_size = jnp.where(x % 2 == 0, 2, jnp.where(x == 1, 4, jnp.where(z % 2 == 0, 8, jnp.where(z % 4 == 1, 16, 32))))
-    top_size = jnp.where(row == N_X * N_Z - 1, 0, top_size)
+    below = jnp.where(z % 2 == 0, 1, jnp.where(z % 4 == 1, 3, jnp.where(z == 3, 3, 0)))
+    upper_half = z // 4
+    top_size = jnp.where(x % 2 == 0, 2, jnp.where(x == 1, 4, 12 + below))
+    relay = jnp.where((y % 2 == 0) & (y != 4), 1, 0)
 
     @pl.when(core == 0)
     def _():
         greet(row, col + 1)
-        greet(sender(TOP, z) * N_X + x, y * 2 + 1)
+        pl.when(upper_half == 0)(lambda: greet(sender(TOP, z) * N_X + x, y * 2 + 1))
+
+        for h in (7, 8, 9):
+            @pl.when((x == 3) & (z != keeper(h)) & ((h < 9) | (upper_half == 0)))
+            def _():
+                greet(keeper(h) * N_X + 3, y * 2)
+
+        @pl.when(row == 15)
+        def _():
+            for i in range(4, 8):
+                greet(i * N_X + 3, y * 2)
 
         @pl.when(y != 7)
         def _():
-            greet(row, 14)
+            greet(row, jnp.where(y % 2 == 0, 7, jnp.where(y == 5, 6, y - 1)) * 2)
 
     @pl.when(core == 1)
     def _():
         greet(row, col - 1)
         for h in (2, 3, 4):
             greet(row, (y - y % 2 ** (h - 1) + 2 ** (h - 2) - 1) * 2)
-        for h in range(2, TOP + 1):
+        for h in range(2, TOP):
             greet(*place(h, sender(h, position(h)), 1))
-        for h in range(5, TOP + 1):
-            greet(row - row % 2 ** (h - 4) + 2 ** (h - 5) - 1, y * 2)
+        pl.when(upper_half == 0)(lambda: greet(*place(TOP, sender(TOP, z), 1)))
+
+        @pl.when((upper_half == 0) & (middle_z == 0))
+        def _():
+            for c in (0, 1):
+                greet(*place(TOP, 7 - z, c))
+                greet(*place(TOP, flip1(7 - z), c))
+
+        for holder in (x - x % 2, 1, 3, 3, 3):
+            greet(z * N_X + holder, y * 2)
 
     receivers = jnp.where(
         core == 0,
-        1 + jnp.where(y == 7, 7, low_size) + top_size,
-        5 + 2 * middle_y + 2 * (1 - middle_y) + 2 * middle_z + 4 * (1 - middle_z),
+        1 + jnp.where(y == 7, 4, low_size) + relay + top_size + upper_half * (1 + x // 3),
+        5 + 2 + 2 * middle_z + upper_half * (4 * (1 - middle_z) + 1),
     )
 
     with jax.named_scope("load"):
@@ -152,6 +177,14 @@
 
     with jax.named_scope("entry"):
         pl.semaphore_wait(barrier, receivers)
+
+    @pl.when(upper_half == 1)
+    def _():
+        pl.semaphore_signal(rdy_sem, inc=1, device_id=place(TOP, sender(TOP, z), 1), device_id_type=MESH_ID)
+
+        @pl.when((core == 0) & (x == 3))
+        def _():
+            pl.semaphore_signal(mrdy_sem, inc=1, device_id=(15, y * 2), device_id_type=MESH_ID)
 
     def remote(src, dst, ssem, rsem, r, c):
         return pltpu.make_async_remote_copy(
@@ -213,8 +246,8 @@
             lambda: (remote(src.at[pl.ds(0, 2)], t_pq.at[h], sem.at[0], rpq_sem.at[h], r, c),),
             lambda: (remote(src.at[pl.ds(2, 2)], t_sw.at[h], sem.at[1], rsw_sem.at[h], r, c),),
             lambda: (
-                remote(src.at[4 + side], t_k.at[h, 0], sem.at[2], rk_sem.at[h], r, c),
-                remote(src.at[7 - side], t_k.at[h, 1], sem.at[2], rk_sem.at[h], r, c),
+                remote(src.at[4 if side is None else 4 + side], t_k.at[h, 0], sem.at[2], rk_sem.at[h], r, c),
+                remote(src.at[5 if side is None else 7 - side], t_k.at[h, 1], sem.at[2], rk_sem.at[h], r, c),
             ),
         )
 
@@ -242,6 +275,9 @@
         def _():
             for c in hand_over(low, low_sem):
                 c.start()
+
+        ahead = remote(vasc.at[3], t_pq.at[2], hd_sem, rpq_sem.at[2], row, me_c + 2)
+        pl.when(y % 2 == 0)(lambda: ahead.start())
 
         down = {}
 
@@ -260,6 +296,7 @@
                 right = mm(right, down["w"])
             if h == TOP:
                 return left, right
+            arrived(r_f.at[h], rf_sem.at[h], f"wait_f{h}")
             g = mm(mm(left, r_f[h]), right)
             down["g"] = g if h == 2 else down["g"] + g
 
@@ -282,8 +319,6 @@
                 compose(3)
             if h == 8:
                 compose(4)
-                compose(5)
-                compose(6)
 
         arrived(r_f.at[1], rf_sem.at[1])
         arrived(r_t.at[1], rt_sem.at[1], "wait_t1")
@@ -293,11 +328,11 @@
             s_f[h] = current.astype(BF)
             if h == TOP:
                 def go():
+                    pl.when(upper_half == 0)(lambda: pl.semaphore_wait(rdy_sem, 4))
                     for p, c in ((far, 1), (near, 1), (far, 0), (near, 0)):
                         send_f(h, p, c).start()
                 when(cond, go)
                 break
-            when(cond, lambda: send_f(h, near if far is None else far, 1).start())
             arrived(t_pq.at[h - 1], rpq_sem.at[h - 1], f"wait_pq{h - 1}")
             term = mm(mm_t0(t_pq[h - 1, 0], current), t_pq[h - 1, 1])
             s_t[h] = term.astype(BF)
@@ -307,15 +342,17 @@
                     send_t(h, far).start()
                 send_t(h, near).start()
                 if far is not None:
-                    send_f(h, near, 1).start()
+                    send_f(h, far, 1).start()
+                send_f(h, near, 1).start()
             when(cond, go)
             with jax.named_scope(f"fill{h}"):
                 filler(h)
             arrived(r_t.at[h], rt_sem.at[h], f"wait_t{h}")
             current = term + r_t[h].astype(F32)
-            if h == 4:
+            if h == GO:
                 pl.semaphore_signal(go_sem, inc=1, device_id=(row, me_c - 1), device_id_type=MESH_ID)
-            arrived(r_f.at[h], rf_sem.at[h], f"wait_f{h}")
+        compose(5)
+        compose(6)
         compose(7)
         compose(8)
         left, right = compose(9)
@@ -326,6 +363,7 @@
         fin.start()
         finish(down["g"], left, right)
         send.wait_send()
+        pl.when(y % 2 == 0)(lambda: ahead.wait_send())
         fin.wait_send()
         sent(low, hs_sem.at[0])
         for h in range(2, TOP + 1):
@@ -366,7 +404,7 @@
             for h in (2, 3, 4):
                 @pl.when(y % 2 ** (h - 1) == 2 ** (h - 2) - 1)
                 def _():
-                    for c in low_copies(h):
+                    for c in list(low_copies(h))[:1 if h == 2 else None]:
                         c[0]()[0].start()
 
         def low_rest():
@@ -387,12 +425,30 @@
                 top.at[parts[k]], top.at[parts[k]], y_sem.at[k], top_sem.at[k], row, j * 2
             )
 
-        def owns(h):
-            return row % 2 ** (h - 4) == 2 ** (h - 5) - 1
-
-        def plane_copy(h, i):
-            size = 2 ** (h - 4)
-            return table_copies(top, tab_sem, h, row - row % size + i, peer, i // (size // 2))
+        def holds(h):
+            return x % 2 == 0 if h == 5 else x == 1 if h == 6 else x == 3
+
+        def along_x(h, k, src, side):
+            first = x if h == 5 else 0
+            for i in range(2 if h == 5 else 4):
+                half = {5: i, 6: i // 2}.get(h, side)
+                for d in table_copies(src, tab_sem.at[h - 5], h, z * N_X + first + i, peer, half)[k]():
+                    yield d
+
+        def along_z(h, k, places=None):
+            size = 2 ** (h - 6)
+            slots = mid.at[h - 7]
+            for i in places or range(min(size, 4)):
+                if i == size // 2 - 1:
+                    continue
+                to = ((z - z % size + i) * N_X + 3, y * 2)
+                sems = (tab_sem.at[h - 5, k], mid_sem.at[h - 7, k])
+                if k < 2:
+                    yield remote(top.at[parts[k]], slots.at[parts[k]], *sems, *to)
+                else:
+                    side = i // (size // 2)
+                    yield remote(top.at[4 + side], slots.at[4], *sems, *to)
+                    yield remote(top.at[7 - side], slots.at[5], *sems, *to)
 
         def upper(k, heights):
             here = (row % 8 != 7) if heights[0] == 5 else (row % 8 == 7) & (row != 31)
@@ -403,17 +459,29 @@
 
                 @pl.when(y == 7)
                 def _():
-                    for j in (3, 4, 2, 5, 1, 0, 6):
+                    for j in (2, 4, 0, 6):
                         ring_copy(k, j).start()
 
+                @pl.when(relay == 1)
+                def _():
+                    ring_copy(k, jnp.where(y == 6, 5, y + 1)).start()
+
                 for h in heights:
-                    @pl.when(owns(h))
+                    @pl.when(holds(h) if h < 7 else holds(h) & (z == keeper(h)))
                     def _():
-                        def body(i, carry):
-                            for d in plane_copy(h, i)[k]():
+                        if h >= 7:
+                            for d in along_z(h, k):
                                 d.start()
-                            return carry
-                        lax.fori_loop(0, 2 ** (h - 4), body, 0)
+                        for d in along_x(h, k, top, 0):
+                            d.start()
+
+        def onward(k, h):
+            @pl.when((x == 3) & (z != keeper(h)))
+            def _():
+                part = pl.ds(4, 2) if k == 2 else parts[k]
+                arrived(mid.at[h - 7, part], mid_sem.at[h - 7, k], f"wait_mid{h}")
+                for d in along_x(h, k, mid.at[h - 7], None):
+                    d.start()
 
         def first_tables():
             upper(0, (5, 6, 7))
@@ -443,9 +511,21 @@
 
         with jax.named_scope("go"):
             pl.semaphore_wait(go_sem, 1)
+        pl.when(y != 7)(low_rest)
+        onward(0, 7)
+
+        @pl.when(row == 15)
+        def _():
+            pl.semaphore_wait(mrdy_sem, 4)
+            for d in along_z(9, 2, range(4, 8)):
+                d.start()
+
+        onward(2, 8)
+        onward(2, 9)
         upper(2, (5, 6, 7))
-        pl.when(y != 7)(low_rest)
+        onward(2, 7)
         upper(1, (5, 6, 7))
+        onward(1, 7)
 
         arrived(r_fin, fr_sem, "wait_fin")
         finish(r_fin[2], r_fin[0], r_fin[1])
@@ -459,7 +539,7 @@
                 @pl.when(y % 2 ** (h - 1) == 2 ** (h - 2) - 1)
                 def _():
                     for k in range(3):
-                        sent(acc.at[0, pl.ds(0, 32 * 2 ** (h - 1))], lows_sem.at[k])
+                        sent(acc.at[0, pl.ds(0, 32 * (1 if (h, k) == (2, 0) else 2 ** (h - 1)))], lows_sem.at[k])
 
         def drained(k, heights):
             here = (row % 8 != 7) if heights[0] == 5 else (row % 8 == 7) & (row != 31)
@@ -468,15 +548,26 @@
             def _():
                 @pl.when(y == 7)
                 def _():
-                    sent(acc.at[0, pl.ds(0, 32 * 7 * (2 if k == 2 else 1))], y_sem.at[k])
-
-                for h in heights:
-                    @pl.when(owns(h))
+                    sent(acc.at[0, pl.ds(0, 32 * 4 * (2 if k == 2 else 1))], y_sem.at[k])
+
+                @pl.when(relay == 1)
+                def _():
+                    sent(acc.at[0, pl.ds(0, 32 * (2 if k == 2 else 1))], y_sem.at[k])
+
+            for h in heights:
+                if h < 7:
+                    @pl.when(holds(h))
                     def _():
-                        if h == 9:
-                            sent(acc, tab_sem.at[k])
-                        else:
-                            sent(acc.at[0, pl.ds(0, 32 * 2 ** (h - 4))], tab_sem.at[k])
+                        sent(acc.at[0, pl.ds(0, 32 * (2 if h == 5 else 4))], tab_sem.at[h - 5, k])
+                    continue
+
+                @pl.when((x == 3) & (z == keeper(h)))
+                def _():
+                    sent(acc.at[0, pl.ds(0, 32 * (4 + 2 ** (h - 6) - 1))], tab_sem.at[h - 5, k])
+
+                @pl.when((x == 3) & (z != keeper(h)))
+                def _():
+                    sent(acc.at[0, pl.ds(0, 32 * 4)], tab_sem.at[h - 5, k])
 
         drained(0, (5, 6, 7))
         drained(1, (5, 6, 7))
@@ -523,6 +614,7 @@
             pltpu.VMEM((10, 2, *tile), BF),
             pltpu.VMEM((8, *tile), BF),
             pltpu.VMEM((8, *tile), BF),
+            pltpu.VMEM((3, 6, *tile), BF),
             pltpu.VMEM((3, *tile), F32),
             pltpu.VMEM((3, *tile), F32),
             dma((7,)),
@@ -536,13 +628,17 @@
             dma((1,)),
             dma((3,)),
             dma((3,)),
+            dma((3, 3)),
             dma((3,)),
-            dma((3,)),
+            dma((5, 3)),
             dma((3,)),
             dma((6,)),
             dma,
             dma,
             pltpu.SemaphoreType.REGULAR,
+            pltpu.SemaphoreType.REGULAR,
+            pltpu.SemaphoreType.REGULAR,
+            dma,
         ],
         compiler_params=pltpu.CompilerParams(collective_id=0, has_side_effects=True),
         name="tree",

time: 47.2 us -> 42.9 us (0.909)
  the two profiles are of different devices: /device:TPU:58 before, /device:TPU:1 now
where the time goes in v3:
time: 42.9 us; the launch traced here: 42.7 us
  Pallas kernels  40.4 us (94%)
  local copies, waits for them, and re-layouts  2.26 us (5%)
    pallas_call x1, Pallas kernels, shards(): pl.pallas_call(kernel, out_shape=jax.ShapeDtypeStruct((2, 512, 512), BF),...  40.4 us
    unnamed x1, local copies, waits for them, and re-layouts  2.26 us

profile of v3, /device:TPU:1, one launch (start us, length us, event | category | flops | bytes accessed | tf_op | source)
XLA Modules:
  0.0 42.7 jit_solution(13490330415651573072)
XLA Ops:
  0.0 40.4 %tree.1 = bf16[2,512,512]{2,1,0:T(8,128)(2,1)} custom-call(bf16[2,512,512]{2,1,0:T(8,128)(2,1)} %da.1, bf16[2,512,512]{2,1,0:T(8,128)(2,1)} %db.1, bf16[2,2,512,128]{3,2,1,0:T(8,128)(2,1)} %ib.1, bf16[2,2,512,128]{3,2,1,0:T(8,128)(2,1)} %ob.1, bf16[1,4,2,128,128]{4,3,2,1,0:T(8,128)(2,1)} %asc.1, bf16[1,4,2,128,128]{4,3,2,1,0:T(8,128)(2,1)} %desc.1, ...), custom_call_target="tpu_custom_call" | custom-call | tf_op jit(solution)/shard_map/tree/pallas_call | solution.py:591
  40.5 2.3 %copy.9 = bf16[2,512,512]{2,1,0:T(8,128)(2,1)} copy(bf16[2,512,512]{2,1,0:T(8,128)(2,1)} %tree.1) | data formatting | bytes 2097152

commit v4 on v3

--- a/solution.py
+++ b/solution.py
@@ -56,9 +56,9 @@
 def kernel(
     da, db, ib, ob, asc, desc, cp, out,
     va, vb, vib, vob, vasc, vdesc, vcp,
-    acc, obuf, us, vw, s_f, s_t, r_f, r_t,
+    acc, us, vw, s_f, s_t, r_f, r_t,
     t_pq, t_sw, t_k, low, top, mid, s_fin, r_fin,
-    ld_sem, st_sem, xs_sem, rf_sem, rt_sem, rpq_sem, rsw_sem, rk_sem,
+    ld_sem, xs_sem, rf_sem, rt_sem, rpq_sem, rsw_sem, rk_sem,
     hs_sem, low_sem, top_sem, mid_sem, y_sem, tab_sem, lows_sem, own_sem, fs_sem, fr_sem, go_sem, rdy_sem, mrdy_sem, hd_sem,
 ):
     row = lax.axis_index("row")
@@ -107,7 +107,8 @@
     pairs = ((ib, vib), (asc.at[0], vasc), (desc.at[0], vdesc), (cp.at[0], vcp), (ob, vob), (da, va), (db, vb))
     for i, (src, dst) in enumerate(pairs):
         c = pltpu.make_async_copy(src, dst, ld_sem.at[i])
-        c.start()
+        if i < 4:
+            c.start()
         loads.append(c)
 
     barrier = pltpu.get_barrier_semaphore()
@@ -145,7 +146,9 @@
     def _():
         greet(row, col - 1)
         for h in (2, 3, 4):
-            greet(row, (y - y % 2 ** (h - 1) + 2 ** (h - 2) - 1) * 2)
+            keeps = y - y % 2 ** (h - 1) + 2 ** (h - 2) - 1
+            greet(row, keeps * 2)
+            pl.when(keeps != y)(lambda: greet(row, keeps * 2 + 1))
         for h in range(2, TOP):
             greet(*place(h, sender(h, position(h)), 1))
         pl.when(upper_half == 0)(lambda: greet(*place(TOP, sender(TOP, z), 1)))
@@ -162,18 +165,20 @@
     receivers = jnp.where(
         core == 0,
         1 + jnp.where(y == 7, 4, low_size) + relay + top_size + upper_half * (1 + x // 3),
-        5 + 2 + 2 * middle_z + upper_half * (4 * (1 - middle_z) + 1),
+        5 + 2 + jnp.where(y == 7, 0, low_size - 1) + 2 * middle_z + upper_half * (4 * (1 - middle_z) + 1),
     )
 
     with jax.named_scope("load"):
+        loads[1].wait()
+        up = [mm(vasc[i, 0], vasc[2, 0]) for i in range(2)], [mm(vasc[i, 1], vasc[2, 1]) for i in range(2)]
         loads[0].wait()
-        loads[1].wait()
+        for c in loads[4:]:
+            c.start()
     leaf = [mm_t0(vib[i, 0], vib[i, 1]) for i in range(2)]
-    term = [mm(mm_t0(vasc[i, 0], leaf[i]), vasc[i, 1]) for i in range(2)]
-    node = term[0] + term[1]
-    lifted = mm(mm_t0(vasc[2, 0], node), vasc[2, 1])
+    lifted = sum(mm(mm_t0(up[0][i], leaf[i]), up[1][i]) for i in range(2))
+    s_t[1] = lifted.astype(BF)
+    node = sum(mm(mm_t0(vasc[i, 0], leaf[i]), vasc[i, 1]) for i in range(2))
     s_f[1] = node.astype(BF)
-    s_t[1] = lifted.astype(BF)
 
     with jax.named_scope("entry"):
         pl.semaphore_wait(barrier, receivers)
@@ -221,11 +226,7 @@
             for r in range(2):
                 rows = pl.ds(r * 256, 256)
                 block = acc[i, rows, :] + mm_t1(spread[r * 256:(r + 1) * 256], vw[i])
-                obuf[i, rows, :] = block.astype(BF)
-                c = pltpu.make_async_copy(obuf.at[i, rows], out.at[i, rows], st_sem)
-                c.start()
-        with jax.named_scope("stores"):
-            pltpu.make_async_copy(obuf, out, st_sem).wait()
+                out[i, rows, :] = block.astype(BF)
 
     def when(cond, f):
         if cond is None:
@@ -266,19 +267,35 @@
                 remote(vcp.at[1], dst.at[pl.ds(4, 4)], hs_sem.at[0], sems.at[2], row, me_c - 1),
             ]
 
-        @pl.when(y == 7)
-        def _():
-            for c in hand_over(top, top_sem):
-                c.start()
-
-        @pl.when(y != 7)
-        def _():
-            for c in hand_over(low, low_sem):
-                c.start()
-
-        ahead = remote(vasc.at[3], t_pq.at[2], hd_sem, rpq_sem.at[2], row, me_c + 2)
-        pl.when(y % 2 == 0)(lambda: ahead.start())
-
+        def hand_all():
+            @pl.when(y == 7)
+            def _():
+                for c in hand_over(top, top_sem):
+                    c.start()
+
+            @pl.when(y != 7)
+            def _():
+                for c in hand_over(low, low_sem)[1:]:
+                    c.start()
+
+        def ahead(h):
+            size = 2 ** (h - 1)
+            base = y - y % size
+            order = {2: (1,), 3: (3, 0, 2), 4: (7, 0, 6, 1, 5, 2, 4)}[h]
+            own = pltpu.make_async_copy(vasc.at[3], t_pq.at[h], rpq_sem.at[h])
+            return own, [
+                remote(vasc.at[3], t_pq.at[h], hd_sem, rpq_sem.at[h], row, (base + i) * 2 + 1) for i in order
+            ]
+
+        for h in (2, 3, 4):
+            @pl.when(y % 2 ** (h - 1) == 2 ** (h - 2) - 1)
+            def _():
+                own, others = ahead(h)
+                for c in others:
+                    c.start()
+                own.start()
+
+        hand_all()
         down = {}
 
         def compose(h):
@@ -363,9 +380,13 @@
         fin.start()
         finish(down["g"], left, right)
         send.wait_send()
-        pl.when(y % 2 == 0)(lambda: ahead.wait_send())
+        for h in (2, 3, 4):
+            @pl.when(y % 2 ** (h - 1) == 2 ** (h - 2) - 1)
+            def _():
+                sent(acc.at[0, pl.ds(0, 32 * (2 ** (h - 1) - 1))], hd_sem)
         fin.wait_send()
-        sent(low, hs_sem.at[0])
+        pl.when(y == 7)(lambda: sent(top, hs_sem.at[0]))
+        pl.when(y != 7)(lambda: sent(low.at[pl.ds(2, 6)], hs_sem.at[0]))
         for h in range(2, TOP + 1):
             cond, near, far = route(h)
             count = 2 if far is None else 4
@@ -398,15 +419,6 @@
             for i in range(size):
                 yield table_copies(low, lows_sem, h, row, (base + i) * 2 + 1, i // (size // 2))
 
-        @pl.when(y != 7)
-        def _():
-            arrived(low.at[pl.ds(0, 2)], low_sem.at[0], "wait_low")
-            for h in (2, 3, 4):
-                @pl.when(y % 2 ** (h - 1) == 2 ** (h - 2) - 1)
-                def _():
-                    for c in list(low_copies(h))[:1 if h == 2 else None]:
-                        c[0]()[0].start()
-
         def low_rest():
             arrived(low.at[pl.ds(2, 2)], low_sem.at[1])
             arrived(low.at[pl.ds(4, 4)], low_sem.at[2])
@@ -538,8 +550,8 @@
             for h in (2, 3, 4):
                 @pl.when(y % 2 ** (h - 1) == 2 ** (h - 2) - 1)
                 def _():
-                    for k in range(3):
-                        sent(acc.at[0, pl.ds(0, 32 * (1 if (h, k) == (2, 0) else 2 ** (h - 1)))], lows_sem.at[k])
+                    for k in (1, 2):
+                        sent(acc.at[0, pl.ds(0, 32 * 2 ** (h - 1))], lows_sem.at[k])
 
         def drained(k, heights):
             here = (row % 8 != 7) if heights[0] == 5 else (row % 8 == 7) & (row != 31)
@@ -585,14 +597,13 @@
 
 
 def shards(dense_a, dense_b, inner, outer, ascent, descent, couplings):
-    any_spec = pl.BlockSpec(memory_space=pl.ANY)
     dma = pltpu.SemaphoreType.DMA
     tile = (128, 128)
     return pl.pallas_call(
         kernel,
-        out_shape=jax.ShapeDtypeStruct((2, 512, 512), BF),
-        in_specs=[any_spec] * 7,
-        out_specs=any_spec,
+        out_shape=pltpu.VMEM((2, 512, 512), BF),
+        in_specs=[pl.BlockSpec(memory_space=pltpu.HBM)] * 7,
+        out_specs=pl.BlockSpec(memory_space=pltpu.VMEM),
         scratch_shapes=[
             pltpu.VMEM((2, 512, 512), BF),
             pltpu.VMEM((2, 512, 512), BF),
@@ -602,7 +613,6 @@
             pltpu.VMEM((4, 2, *tile), BF),
             pltpu.VMEM((2, 4, *tile), BF),
             pltpu.VMEM((2, 512, 512), F32),
-            pltpu.VMEM((2, 512, 512), BF),
             pltpu.VMEM((2, 512, 128), BF),
             pltpu.VMEM((2, 512, 128), BF),
             pltpu.VMEM((10, *tile), BF),
@@ -618,7 +628,6 @@
             pltpu.VMEM((3, *tile), F32),
             pltpu.VMEM((3, *tile), F32),
             dma((7,)),
-            dma,
             dma((10,)),
             dma((10,)),
             dma((10,)),
@@ -640,9 +649,9 @@
             pltpu.SemaphoreType.REGULAR,
             dma,
         ],
-        compiler_params=pltpu.CompilerParams(collective_id=0, has_side_effects=True),
+        compiler_params=pltpu.CompilerParams(collective_id=0, has_side_effects=True, vmem_limit_bytes=24 * 2**20),
         name="tree",
-    )(dense_a, dense_b, inner, outer, ascent, descent, couplings)
+    )(*[pltpu.with_memory_space_constraint(v, pltpu.HBM) for v in (dense_a, dense_b, inner, outer, ascent, descent, couplings)])
 
 
 def solution(mesh):

time: 42.9 us -> 40.8 us (0.951)
  local copies, waits for them, and re-layouts: 2.26 us -> 0.97 us
  Pallas kernels: 40.4 us -> 39.7 us
    unnamed x1, local copies, waits for them, and re-layouts: 2.26 us -> 0.97 us
    pallas_call x1, Pallas kernels: 40.4 us -> 39.7 us  [shards(): pl.pallas_call(kernel, out_shape=pltpu.VMEM((2, 512, 512), BF), in_specs=...]
where the time goes in v4:
time: 40.8 us; the launch traced here: 40.7 us
  Pallas kernels  39.7 us (97%)
  local copies, waits for them, and re-layouts  0.97 us (2%)
    pallas_call x1, Pallas kernels, shards(): pl.pallas_call(kernel, out_shape=pltpu.VMEM((2, 512, 512), BF), in_specs=...  39.7 us
    unnamed x1, local copies, waits for them, and re-layouts  0.97 us

profile of v4, /device:TPU:1, one launch (start us, length us, event | category | flops | bytes accessed | tf_op | source)
XLA Modules:
  0.0 40.7 jit_solution(3266999993830817275)
XLA Ops:
  0.0 39.7 %tree.1 = bf16[2,512,512]{2,1,0:T(8,128)(2,1)S(1)} custom-call(bf16[2,512,512]{2,1,0:T(8,128)(2,1)} %da.1, bf16[2,512,512]{2,1,0:T(8,128)(2,1)} %db.1, bf16[2,2,512,128]{3,2,1,0:T(8,128)(2,1)} %ib.1, bf16[2,2,512,128]{3,2,1,0:T(8,128)(2,1)} %ob.1, bf16[1,4,2,128,128]{4,3,2,1,0:T(8,128)(2,1)} %asc.1, bf16[1,4,2,128,128]{4,3,2,1,0:T(8,128)(2,1)} %desc.1, ...), custom_call_target="tpu_custom_call" | custom-call | tf_op jit(solution)/shard_map/tree/pallas_call | solution.py:602
  39.7 1.0 %copy.9 = bf16[2,512,512]{2,1,0:T(8,128)(2,1)} copy(bf16[2,512,512]{2,1,0:T(8,128)(2,1)S(1)} %tree.1) | data formatting | bytes 2097152

commit v5 on v4

--- a/solution.py
+++ b/solution.py
@@ -56,7 +56,7 @@
 def kernel(
     da, db, ib, ob, asc, desc, cp, out,
     va, vb, vib, vob, vasc, vdesc, vcp,
-    acc, us, vw, s_f, s_t, r_f, r_t,
+    acc, us, vw, bw, s_f, s_t, r_f, r_t,
     t_pq, t_sw, t_k, low, top, mid, s_fin, r_fin,
     ld_sem, xs_sem, rf_sem, rt_sem, rpq_sem, rsw_sem, rk_sem,
     hs_sem, low_sem, top_sem, mid_sem, y_sem, tab_sem, lows_sem, own_sem, fs_sem, fr_sem, go_sem, rdy_sem, mrdy_sem, hd_sem,
@@ -106,10 +106,9 @@
     loads = []
     pairs = ((ib, vib), (asc.at[0], vasc), (desc.at[0], vdesc), (cp.at[0], vcp), (ob, vob), (da, va), (db, vb))
     for i, (src, dst) in enumerate(pairs):
-        c = pltpu.make_async_copy(src, dst, ld_sem.at[i])
-        if i < 4:
-            c.start()
-        loads.append(c)
+        loads.append(pltpu.make_async_copy(src, dst, ld_sem.at[i]))
+    for i in (1, 0):
+        loads[i].start()
 
     barrier = pltpu.get_barrier_semaphore()
 
@@ -172,7 +171,7 @@
         loads[1].wait()
         up = [mm(vasc[i, 0], vasc[2, 0]) for i in range(2)], [mm(vasc[i, 1], vasc[2, 1]) for i in range(2)]
         loads[0].wait()
-        for c in loads[4:]:
+        for c in loads[2:]:
             c.start()
     leaf = [mm_t0(vib[i, 0], vib[i, 1]) for i in range(2)]
     lifted = sum(mm(mm_t0(up[0][i], leaf[i]), up[1][i]) for i in range(2))
@@ -218,14 +217,19 @@
             vw[i] = mm(vob[i, 1], mm(vdesc[i, 1], vdesc[2, 1])).astype(BF)
             acc[i] += mm_t1(mm(vob[i, 0], g.astype(BF)).astype(BF), vob[i, 1])
 
-    def finish(g, left, right):
+    def prepare(g, left, right):
+        for i in range(2):
+            acc[i] += mm_t1(mm(us[i], g.astype(BF)).astype(BF), vw[i])
+            us[i] = mm(us[i], left).astype(BF)
+            bw[i] = mm_t1(right, vw[i]).astype(BF)
+
+    def finish():
         arrived(r_f.at[TOP], rf_sem.at[TOP], "wait_f9")
-        g = (g + mm(mm(left, r_f[TOP]), right)).astype(BF)
         for i in range(2):
-            spread = mm(us[i], g).astype(BF)
+            spread = mm(us[i], r_f[TOP]).astype(BF)
             for r in range(2):
                 rows = pl.ds(r * 256, 256)
-                block = acc[i, rows, :] + mm_t1(spread[r * 256:(r + 1) * 256], vw[i])
+                block = acc[i, rows, :] + mm(spread[r * 256:(r + 1) * 256], bw[i])
                 out[i, rows, :] = block.astype(BF)
 
     def when(cond, f):
@@ -287,14 +291,16 @@
                 remote(vasc.at[3], t_pq.at[h], hd_sem, rpq_sem.at[h], row, (base + i) * 2 + 1) for i in order
             ]
 
-        for h in (2, 3, 4):
-            @pl.when(y % 2 ** (h - 1) == 2 ** (h - 2) - 1)
-            def _():
-                own, others = ahead(h)
-                for c in others:
-                    c.start()
-                own.start()
-
+        def spread_ahead(heights):
+            for h in heights:
+                @pl.when(y % 2 ** (h - 1) == 2 ** (h - 2) - 1)
+                def _():
+                    own, others = ahead(h)
+                    for c in others:
+                        c.start()
+                    own.start()
+
+        spread_ahead((2,))
         hand_all()
         down = {}
 
@@ -346,12 +352,15 @@
             if h == TOP:
                 def go():
                     pl.when(upper_half == 0)(lambda: pl.semaphore_wait(rdy_sem, 4))
-                    for p, c in ((far, 1), (near, 1), (far, 0), (near, 0)):
+                    for p, c in ((near, 1), (near, 0), (far, 1), (far, 0)):
                         send_f(h, p, c).start()
                 when(cond, go)
                 break
-            arrived(t_pq.at[h - 1], rpq_sem.at[h - 1], f"wait_pq{h - 1}")
-            term = mm(mm_t0(t_pq[h - 1, 0], current), t_pq[h - 1, 1])
+            if h == 2:
+                arrived(t_pq.at[1], rpq_sem.at[1], "wait_pq1")
+                term = mm(mm_t0(t_pq[1, 0], current), t_pq[1, 1])
+            else:
+                term = mm(mm(turned, current), t_pq[h - 1, 1])
             s_t[h] = term.astype(BF)
 
             def go():
@@ -362,8 +371,13 @@
                     send_f(h, far, 1).start()
                 send_f(h, near, 1).start()
             when(cond, go)
+            if h == 2:
+                spread_ahead((3, 4))
             with jax.named_scope(f"fill{h}"):
                 filler(h)
+            if h < TOP - 1:
+                arrived(t_pq.at[h], rpq_sem.at[h], f"wait_pq{h}")
+                turned = t_pq[h, 0].T
             arrived(r_t.at[h], rt_sem.at[h], f"wait_t{h}")
             current = term + r_t[h].astype(F32)
             if h == GO:
@@ -378,7 +392,7 @@
         s_fin[2] = down["g"]
         fin = remote(s_fin, r_fin, fs_sem, fr_sem, row, me_c - 1)
         fin.start()
-        finish(down["g"], left, right)
+        prepare(down["g"], left, right)
         send.wait_send()
         for h in (2, 3, 4):
             @pl.when(y % 2 ** (h - 1) == 2 ** (h - 2) - 1)
@@ -391,6 +405,7 @@
             cond, near, far = route(h)
             count = 2 if far is None else 4
             when(cond, lambda: sent(s_f.at[pl.ds(0, count)], xs_sem.at[h]))
+        finish()
 
     @pl.when(core == 0)
     def _():
@@ -540,7 +555,7 @@
         onward(1, 7)
 
         arrived(r_fin, fr_sem, "wait_fin")
-        finish(r_fin[2], r_fin[0], r_fin[1])
+        prepare(r_fin[2], r_fin[0], r_fin[1])
 
         for c in mine:
             c.wait_send()
@@ -594,6 +609,8 @@
         @pl.when((y == 7) & (row == 31))
         def _():
             arrived(top.at[parts[2]], top_sem.at[2])
+
+        finish()
 
 
 def shards(dense_a, dense_b, inner, outer, ascent, descent, couplings):
@@ -615,6 +632,7 @@
             pltpu.VMEM((2, 512, 512), F32),
             pltpu.VMEM((2, 512, 128), BF),
             pltpu.VMEM((2, 512, 128), BF),
+            pltpu.VMEM((2, 128, 512), BF),
             pltpu.VMEM((10, *tile), BF),
             pltpu.VMEM((10, *tile), BF),
             pltpu.VMEM((10, *tile), BF),

time: 40.8 us -> 39.5 us (0.968)
  Pallas kernels: 39.7 us -> 38.2 us
    pallas_call x1, Pallas kernels: 39.7 us -> 38.2 us  [shards(): pl.pallas_call(kernel, out_shape=pltpu.VMEM((2, 512, 512), BF), in_specs=...]
where the time goes in v5:
time: 39.5 us; the launch traced here: 39.2 us
  Pallas kernels  38.2 us (97%)
  local copies, waits for them, and re-layouts  0.97 us (2%)
    pallas_call x1, Pallas kernels, shards(): pl.pallas_call(kernel, out_shape=pltpu.VMEM((2, 512, 512), BF), in_specs=...  38.2 us
    unnamed x1, local copies, waits for them, and re-layouts  0.97 us

profile of v5, /device:TPU:1, one launch (start us, length us, event | category | flops | bytes accessed | tf_op | source)
XLA Modules:
  0.0 39.2 jit_solution(9850366070383339339)
XLA Ops:
  0.0 38.2 %tree.1 = bf16[2,512,512]{2,1,0:T(8,128)(2,1)S(1)} custom-call(bf16[2,512,512]{2,1,0:T(8,128)(2,1)} %da.1, bf16[2,512,512]{2,1,0:T(8,128)(2,1)} %db.1, bf16[2,2,512,128]{3,2,1,0:T(8,128)(2,1)} %ib.1, bf16[2,2,512,128]{3,2,1,0:T(8,128)(2,1)} %ob.1, bf16[1,4,2,128,128]{4,3,2,1,0:T(8,128)(2,1)} %asc.1, bf16[1,4,2,128,128]{4,3,2,1,0:T(8,128)(2,1)} %desc.1, ...), custom_call_target="tpu_custom_call" | custom-call | tf_op jit(solution)/shard_map/tree/pallas_call | solution.py:619
  38.3 1.0 %copy.9 = bf16[2,512,512]{2,1,0:T(8,128)(2,1)} copy(bf16[2,512,512]{2,1,0:T(8,128)(2,1)S(1)} %tree.1) | data formatting | bytes 2097152

commit v6 on v5

--- a/solution.py
+++ b/solution.py
@@ -119,7 +119,7 @@
     low_size = jnp.where(y % 2 == 0, 2, jnp.where(y % 4 == 1, 4, 8))
     below = jnp.where(z % 2 == 0, 1, jnp.where(z % 4 == 1, 3, jnp.where(z == 3, 3, 0)))
     upper_half = z // 4
-    top_size = jnp.where(x % 2 == 0, 2, jnp.where(x == 1, 4, 12 + below))
+    top_size = jnp.where(x <= 2, 4, 12 + below)
     relay = jnp.where((y % 2 == 0) & (y != 4), 1, 0)
 
     @pl.when(core == 0)
@@ -158,13 +158,14 @@
                 greet(*place(TOP, 7 - z, c))
                 greet(*place(TOP, flip1(7 - z), c))
 
-        for holder in (x - x % 2, 1, 3, 3, 3):
+        for holder in (x - x % 2, (x - x % 2 + 2) % 4, 1, 3, 3, 3):
             greet(z * N_X + holder, y * 2)
+        greet(*place(5, 3 - flip1(x), 1))
 
     receivers = jnp.where(
         core == 0,
         1 + jnp.where(y == 7, 4, low_size) + relay + top_size + upper_half * (1 + x // 3),
-        5 + 2 + jnp.where(y == 7, 0, low_size - 1) + 2 * middle_z + upper_half * (4 * (1 - middle_z) + 1),
+        6 + 2 + jnp.where(y == 7, 0, low_size - 1) + 2 * middle_z + upper_half * (4 * (1 - middle_z) + 1),
     )
 
     with jax.named_scope("load"):
@@ -319,7 +320,8 @@
                 right = mm(right, down["w"])
             if h == TOP:
                 return left, right
-            arrived(r_f.at[h], rf_sem.at[h], f"wait_f{h}")
+            if h != 6:
+                arrived(r_f.at[h], rf_sem.at[h], f"wait_f{h}")
             g = mm(mm(left, r_f[h]), right)
             down["g"] = g if h == 2 else down["g"] + g
 
@@ -347,6 +349,8 @@
         arrived(r_t.at[1], rt_sem.at[1], "wait_t1")
         current = lifted + r_t[1].astype(F32)
         for h in range(2, TOP + 1):
+            if h == 6:
+                continue
             cond, near, far = route(h)
             s_f[h] = current.astype(BF)
             if h == TOP:
@@ -356,14 +360,17 @@
                         send_f(h, p, c).start()
                 when(cond, go)
                 break
-            if h == 2:
-                arrived(t_pq.at[1], rpq_sem.at[1], "wait_pq1")
-                term = mm(mm_t0(t_pq[1, 0], current), t_pq[1, 1])
+            if h in (2, 7):
+                arrived(t_pq.at[h - 1], rpq_sem.at[h - 1], f"wait_pq{h - 1}")
+                term = mm(mm_t0(t_pq[h - 1, 0], current), t_pq[h - 1, 1])
             else:
                 term = mm(mm(turned, current), t_pq[h - 1, 1])
             s_t[h] = term.astype(BF)
 
             def go():
+                if h == 5:
+                    for p, slot in ((3 - flip1(x), 0), (3 - x, 6)):
+                        remote(s_t.at[5], r_t.at[slot], xs_sem.at[5], rt_sem.at[slot], *place(5, p, 1)).start()
                 if far is not None:
                     send_t(h, far).start()
                 send_t(h, near).start()
@@ -378,8 +385,17 @@
             if h < TOP - 1:
                 arrived(t_pq.at[h], rpq_sem.at[h], f"wait_pq{h}")
                 turned = t_pq[h, 0].T
+            if h == 5:
+                arrived(t_pq.at[0], rpq_sem.at[0], "wait_pq0")
+                turned_other = t_pq[0, 0].T
             arrived(r_t.at[h], rt_sem.at[h], f"wait_t{h}")
             current = term + r_t[h].astype(F32)
+            if h == 5:
+                arrived(r_t.at[6], rt_sem.at[6], "wait_t6")
+                arrived(r_t.at[0], rt_sem.at[0], "wait_t0")
+                other = r_t[6].astype(F32) + r_t[0].astype(F32)
+                r_f[6] = other.astype(BF)
+                current = mm(mm(turned, current), t_pq[5, 1]) + mm(mm(turned_other, other), t_pq[0, 1])
             if h == GO:
                 pl.semaphore_signal(go_sem, inc=1, device_id=(row, me_c - 1), device_id_type=MESH_ID)
         compose(5)
@@ -403,7 +419,9 @@
         pl.when(y != 7)(lambda: sent(low.at[pl.ds(2, 6)], hs_sem.at[0]))
         for h in range(2, TOP + 1):
             cond, near, far = route(h)
-            count = 2 if far is None else 4
+            if h == 6:
+                continue
+            count = 2 if far is None and h != 5 else 4
             when(cond, lambda: sent(s_f.at[pl.ds(0, count)], xs_sem.at[h]))
         finish()
 
@@ -456,6 +474,12 @@
             return x % 2 == 0 if h == 5 else x == 1 if h == 6 else x == 3
 
         def along_x(h, k, src, side):
+            if (h, k) == (5, 0):
+                for i in range(4):
+                    slot = jnp.where(x // 2 == i // 2, 5, 0)
+                    for d in table_copies(src, tab_sem.at[0], slot, z * N_X + i, peer, 0)[0]():
+                        yield d
+                return
             first = x if h == 5 else 0
             for i in range(2 if h == 5 else 4):
                 half = {5: i, 6: i // 2}.get(h, side)
@@ -585,7 +609,7 @@
                 if h < 7:
                     @pl.when(holds(h))
                     def _():
-                        sent(acc.at[0, pl.ds(0, 32 * (2 if h == 5 else 4))], tab_sem.at[h - 5, k])
+                        sent(acc.at[0, pl.ds(0, 32 * (2 if h == 5 and k else 4))], tab_sem.at[h - 5, k])
                     continue
 
                 @pl.when((x == 3) & (z == keeper(h)))

time: 39.5 us -> 39 us (0.987)
  Pallas kernels: 38.2 us -> 37.8 us
    pallas_call x1, Pallas kernels: 38.2 us -> 37.8 us  [shards(): pl.pallas_call(kernel, out_shape=pltpu.VMEM((2, 512, 512), BF), in_specs=...]
where the time goes in v6:
time: 39 us; the launch traced here: 38.8 us
  Pallas kernels  37.8 us (97%)
  local copies, waits for them, and re-layouts  0.97 us (2%)
    pallas_call x1, Pallas kernels, shards(): pl.pallas_call(kernel, out_shape=pltpu.VMEM((2, 512, 512), BF), in_specs=...  37.8 us
    unnamed x1, local copies, waits for them, and re-layouts  0.97 us

profile of v6, /device:TPU:1, one launch (start us, length us, event | category | flops | bytes accessed | tf_op | source)
XLA Modules:
  0.0 38.8 jit_solution(8535639587903219414)
XLA Ops:
  0.0 37.8 %tree.1 = bf16[2,512,512]{2,1,0:T(8,128)(2,1)S(1)} custom-call(bf16[2,512,512]{2,1,0:T(8,128)(2,1)} %da.1, bf16[2,512,512]{2,1,0:T(8,128)(2,1)} %db.1, bf16[2,2,512,128]{3,2,1,0:T(8,128)(2,1)} %ib.1, bf16[2,2,512,128]{3,2,1,0:T(8,128)(2,1)} %ob.1, bf16[1,4,2,128,128]{4,3,2,1,0:T(8,128)(2,1)} %asc.1, bf16[1,4,2,128,128]{4,3,2,1,0:T(8,128)(2,1)} %desc.1, ...), custom_call_target="tpu_custom_call" | custom-call | tf_op jit(solution)/shard_map/tree/pallas_call | solution.py:643
  37.8 1.0 %copy.9 = bf16[2,512,512]{2,1,0:T(8,128)(2,1)} copy(bf16[2,512,512]{2,1,0:T(8,128)(2,1)S(1)} %tree.1) | data formatting | bytes 2097152

commit v7 on v6

--- a/solution.py
+++ b/solution.py
@@ -107,8 +107,11 @@
     pairs = ((ib, vib), (asc.at[0], vasc), (desc.at[0], vdesc), (cp.at[0], vcp), (ob, vob), (da, va), (db, vb))
     for i, (src, dst) in enumerate(pairs):
         loads.append(pltpu.make_async_copy(src, dst, ld_sem.at[i]))
-    for i in (1, 0):
-        loads[i].start()
+    leaf_loads = [
+        pltpu.make_async_copy(ib.at[i, j], vib.at[i, j], ld_sem.at[7 + 2 * i + j]) for i in range(2) for j in range(2)
+    ]
+    for c in (loads[1], *leaf_loads):
+        c.start()
 
     barrier = pltpu.get_barrier_semaphore()
 
@@ -171,7 +174,8 @@
     with jax.named_scope("load"):
         loads[1].wait()
         up = [mm(vasc[i, 0], vasc[2, 0]) for i in range(2)], [mm(vasc[i, 1], vasc[2, 1]) for i in range(2)]
-        loads[0].wait()
+        for c in leaf_loads:
+            c.wait()
         for c in loads[2:]:
             c.start()
     leaf = [mm_t0(vib[i, 0], vib[i, 1]) for i in range(2)]
@@ -669,7 +673,7 @@
             pltpu.VMEM((3, 6, *tile), BF),
             pltpu.VMEM((3, *tile), F32),
             pltpu.VMEM((3, *tile), F32),
-            dma((7,)),
+            dma((11,)),
             dma((10,)),
             dma((10,)),
             dma((10,)),

time: 39 us -> 39 us (level)
  no operation moved by 1% of the time
where the time goes in v7:
time: 39 us; the launch traced here: 38.9 us
  Pallas kernels  37.9 us (97%)
  local copies, waits for them, and re-layouts  0.97 us (2%)
    pallas_call x1, Pallas kernels, shards(): pl.pallas_call(kernel, out_shape=pltpu.VMEM((2, 512, 512), BF), in_specs=...  37.9 us
    unnamed x1, local copies, waits for them, and re-layouts  0.97 us

profile of v7, /device:TPU:1, one launch (start us, length us, event | category | flops | bytes accessed | tf_op | source)
XLA Modules:
  0.0 38.9 jit_solution(16406620065273746133)
XLA Ops:
  0.0 37.9 %tree.1 = bf16[2,512,512]{2,1,0:T(8,128)(2,1)S(1)} custom-call(bf16[2,512,512]{2,1,0:T(8,128)(2,1)} %da.1, bf16[2,512,512]{2,1,0:T(8,128)(2,1)} %db.1, bf16[2,2,512,128]{3,2,1,0:T(8,128)(2,1)} %ib.1, bf16[2,2,512,128]{3,2,1,0:T(8,128)(2,1)} %ob.1, bf16[1,4,2,128,128]{4,3,2,1,0:T(8,128)(2,1)} %asc.1, bf16[1,4,2,128,128]{4,3,2,1,0:T(8,128)(2,1)} %desc.1, ...), custom_call_target="tpu_custom_call" | custom-call | tf_op jit(solution)/shard_map/tree/pallas_call | solution.py:647
  37.9 1.0 %copy.9 = bf16[2,512,512]{2,1,0:T(8,128)(2,1)} copy(bf16[2,512,512]{2,1,0:T(8,128)(2,1)S(1)} %tree.1) | data formatting | bytes 2097152
